TPU v7x, 16 devices: a whole 2x2x2 slice. The times are simulated.
16 devices in a mesh: dp: 2 (over z), tp: 8 (over y, x, core).
Axes of the slice: x: 2, y: 2, z: 2, core: 2. Of those that a mesh axis runs over, the one named last changes fastest.
Arguments:
- out_y1: float32 [16, 1024, 1280], P('dp'), parts along dimension 0
- out_y2: float32 [16, 1024, 1280], P('dp'), parts along dimension 0
- cot_y1: float32 [16, 1024, 1280], P('dp'), parts along dimension 0
- cot_y2: float32 [16, 1024, 1280], P('dp'), parts along dimension 0
- w_qkv: bfloat16 [1, 1280, 16, 3, 80], P(None, None, 'tp')
- w_out: bfloat16 [1, 16, 80, 1280], P(None, 'tp')
- w_up: bfloat16 [1, 1280, 5120], P(None, None, 'tp')
- w_down: bfloat16 [1, 5120, 1280], P(None, 'tp')
Outputs:
- output 1: float32 [16, 1024, 1280], P('dp'), parts along dimension 0
- output 2: float32 [16, 1024, 1280], P('dp'), parts along dimension 0
- output 3: float32 [16, 1024, 1280], P('dp'), parts along dimension 0
- output 4: float32 [16, 1024, 1280], P('dp'), parts along dimension 0
- output 5: float32 [2, 1280, 16, 3, 80], P('dp', None, 'tp'), parts along dimension 0
- output 6: float32 [2, 16, 80, 1280], P('dp', 'tp'), parts along dimension 0
- output 7: float32 [2, 1280, 5120], P('dp', None, 'tp'), parts along dimension 0
- output 8: float32 [2, 5120, 1280], P('dp', 'tp'), parts along dimension 0
There are 2 independent parts. A program takes and returns all parts, laid end to end along the dimension named above; an argument that names none is the same for every part.
All inputs are finite; a program needn't handle non-finite values.
Results may differ from a plain program's by a relative error of at most 0.0124101.
Values are sent between devices in bfloat16 or wider.
A program may use at most 1.5 GiB of HBM per device.

v0:
```python
import math
import jax
import jax.numpy as jnp
from jax import lax
from jax.sharding import PartitionSpec as P

NORM_EPS = 1e-6


def rms_fwd(x_in):
    inv_rms = lax.rsqrt(jnp.mean(x_in * x_in, axis=-1, keepdims=True) + NORM_EPS)
    return inv_rms, x_in * inv_rms


def rms_back(norm_state, grad_n):
    inv_rms, normed = norm_state
    return inv_rms * (grad_n - normed * jnp.mean(normed * grad_n, axis=-1, keepdims=True))


def mlp_forward(x_in, w_up, w_down):
    norm_state = rms_fwd(x_in)
    n_bf = norm_state[1].astype(jnp.bfloat16)
    hidden = jnp.einsum("bsd,df->bsf", n_bf, w_up, preferred_element_type=jnp.float32)
    act_f, gelu_back = jax.vjp(jax.nn.gelu, hidden)
    act_bf = act_f.astype(jnp.bfloat16)
    part_sum = jnp.einsum("bsf,fd->bsd", act_bf, w_down, preferred_element_type=jnp.float32)
    return part_sum, norm_state, (n_bf, act_bf, gelu_back)


def mlp_backward(cot_out, w_up, w_down, saved):
    n_bf, act_bf, gelu_back = saved
    cot_bf = cot_out.astype(jnp.bfloat16)
    g_down = jnp.einsum("bsf,bsd->fd", act_bf, cot_bf, preferred_element_type=jnp.float32)
    grad_act = jnp.einsum("bsd,fd->bsf", cot_bf, w_down, preferred_element_type=jnp.float32)
    grad_hid = gelu_back(grad_act)[0].astype(jnp.bfloat16)
    g_up = jnp.einsum("bsd,bsf->df", n_bf, grad_hid, preferred_element_type=jnp.float32)
    grad_n = jnp.einsum("bsf,df->bsd", grad_hid, w_up, preferred_element_type=jnp.float32)
    return g_up, g_down, grad_n


def attn_forward(x_in, w_qkv, w_out):
    norm_state = rms_fwd(x_in)
    n_bf = norm_state[1].astype(jnp.bfloat16)
    score_scale = 1.0 / math.sqrt(w_qkv.shape[-1])
    qkv = jnp.einsum("bsd,dhje->bshje", n_bf, w_qkv, preferred_element_type=jnp.float32).astype(jnp.bfloat16)
    q_rows = qkv[:, :, :, 0]
    k_rows = qkv[:, :, :, 1]
    v_rows = qkv[:, :, :, 2]
    scores = jnp.einsum("bqhe,bkhe->bhqk", q_rows, k_rows, preferred_element_type=jnp.float32) * score_scale
    attn_prob = jax.nn.softmax(scores, axis=-1)
    prob_bf = attn_prob.astype(jnp.bfloat16)
    attn_out = jnp.einsum("bhqk,bkhe->bqhe", prob_bf, v_rows, preferred_element_type=jnp.float32).astype(jnp.bfloat16)
    part_sum = jnp.einsum("crif,ife->cre", attn_out, w_out, preferred_element_type=jnp.float32)
    return part_sum, norm_state, (n_bf, q_rows, k_rows, v_rows, attn_prob, prob_bf, attn_out)


def attn_backward(cot_out, w_qkv, w_out, saved):
    n_bf, q_rows, k_rows, v_rows, attn_prob, prob_bf, attn_out = saved
    score_scale = 1.0 / math.sqrt(w_qkv.shape[-1])
    cot_bf = cot_out.astype(jnp.bfloat16)
    g_out = jnp.einsum("crif,cre->ife", attn_out, cot_bf, preferred_element_type=jnp.float32)
    grad_o = jnp.einsum("cre,ife->crif", cot_bf, w_out, preferred_element_type=jnp.float32).astype(jnp.bfloat16)
    grad_p = jnp.einsum("bqhe,bkhe->bhqk", grad_o, v_rows, preferred_element_type=jnp.float32)
    grad_v = jnp.einsum("bhqk,bqhe->bkhe", prob_bf, grad_o, preferred_element_type=jnp.float32)
    grad_s = (attn_prob * (grad_p - jnp.sum(grad_p * attn_prob, axis=-1, keepdims=True)) * score_scale).astype(jnp.bfloat16)
    grad_q = jnp.einsum("bhqk,bkhe->bqhe", grad_s, k_rows, preferred_element_type=jnp.float32)
    grad_k = jnp.einsum("bhqk,bqhe->bkhe", grad_s, q_rows, preferred_element_type=jnp.float32)
    grad_qkv = jnp.stack([grad_q, grad_k, grad_v], axis=3).astype(jnp.bfloat16)
    g_qkv = jnp.einsum("bsd,bshje->dhje", n_bf, grad_qkv, preferred_element_type=jnp.float32)
    grad_n = jnp.einsum("bshje,dhje->bsd", grad_qkv, w_qkv, preferred_element_type=jnp.float32)
    return g_qkv, g_out, grad_n


def solution(mesh):
    act_spec = P("dp", None, None)
    weight_specs = (P(None, None, "tp", None, None), P(None, "tp", None, None), P(None, None, "tp"), P(None, "tp", None))
    grad_specs = (P("dp", None, "tp", None, None), P("dp", "tp", None, None), P("dp", None, "tp"), P("dp", "tp", None))

    def local_backward(out_y1, out_y2, cot_y1, cot_y2, w_qkv, w_out, w_up, w_down):
        run_y1, run_y2, run_c1, run_c2 = out_y1, out_y2, cot_y1, cot_y2
        per_layer = []
        for layer_idx in reversed(range(w_qkv.shape[0])):
            g_part, g_norm, g_saved = mlp_forward(run_y1, w_up[layer_idx], w_down[layer_idx])
            low_x2 = run_y2 - lax.psum(g_part, "tp")
            g_up, g_down, gn_part = mlp_backward(run_c2, w_up[layer_idx], w_down[layer_idx], g_saved)
            grad_n = lax.psum(gn_part.astype(jnp.bfloat16), "tp").astype(jnp.float32)
            run_c1 = run_c1 + rms_back(g_norm, grad_n)
            f_part, f_norm, f_saved = attn_forward(low_x2, w_qkv[layer_idx], w_out[layer_idx])
            run_y1 = run_y1 - lax.psum(f_part, "tp")
            g_qkv, g_out, fn_part = attn_backward(run_c1, w_qkv[layer_idx], w_out[layer_idx], f_saved)
            grad_n = lax.psum(fn_part.astype(jnp.bfloat16), "tp").astype(jnp.float32)
            run_c2 = run_c2 + rms_back(f_norm, grad_n)
            run_y2 = low_x2
            per_layer.append((g_qkv, g_out, g_up, g_down))
        per_layer = per_layer[::-1]
        stacked = [jnp.stack([layer_grads[slot_idx] for layer_grads in per_layer]) for slot_idx in range(4)]
        return (run_y1, run_y2, run_c1, run_c2, stacked[0], stacked[1], stacked[2], stacked[3])

    return jax.shard_map(local_backward, mesh=mesh, in_specs=(act_spec, act_spec, act_spec, act_spec) + weight_specs, out_specs=(act_spec, act_spec, act_spec, act_spec) + grad_specs, check_vma=False)
```

profile of v0, /device:TPU:0, one launch (start us, length us, event | category | flops | bytes accessed | tf_op | source)
XLA Modules:
  0.0 1970.3 jit_solution(12890877275647825768)
XLA Ops:
  7.2 0.0 copy-start
  7.2 0.0 copy-start.8
  7.2 0.0 all-reduce.5.cloned.1.call-start
  7.2 16.6 multiply_reduce_fusion.3
  23.8 0.0 copy-start.2
  23.9 28.3 %fusion.51 = f32[8,1024,640]{2,1,0:T(8,128)} fusion(f32[8,1024,1280]{2,1,0:T(8,128)} %param.8, f32[8,1024]{1,0:T(8,128)S(1)} %add_rsqrt_fusion.1, bf16[1,1280,640]{2,1,0:T(8,128)(2,1)S(1)} %copy-done.8), kind=kOutput, calls=%fused_computation.59 | convolution fusion | flops 13442744320 | bytes 64585728 | tf_op jit(solution)/shard_map/bsd,df->bsf/dot_general | solution.py:23
  52.2 30.5 %fusion.87 = f32[8,1024,1280]{2,1,0:T(8,128)} fusion(bf16[1,640,1280]{2,1,0:T(8,128)(2,1)S(1)} %copy-done, f32[8,1024,640]{2,1,0:T(8,128)} %fusion.51), kind=kOutput, calls=%fused_computation.80 | convolution fusion | flops 13468958720 | bytes 64552960 | tf_op jit(solution)/shard_map/bsf,fd->bsd/dot_general | solution.py:26
  82.7 0.0 all-reduce.5.cloned.1.call-update
  82.7 0.0 all-reduce.9.cloned.1.call-start
  82.8 34.6 %fusion.29 = bf16[8,1024,640]{2,1,0:T(8,128)(2,1)} fusion(f32[8,1024,640]{2,1,0:T(8,128)} %fusion.51, f32[8,1024,1280]{2,1,0:T(8,128)} %param.11, bf16[1,640,1280]{2,1,0:T(8,128)(2,1)S(1)} %copy-done), kind=kOutput, calls=%fused_computation.37 | convolution fusion | flops 13537116160 | bytes 75038720 | tf_op jit(solution)/shard_map/bsd,fd->bsf/dot_general | solution.py:34
  117.4 23.4 %convolution_convert_fusion = bf16[8,1024,1280]{2,1,0:T(8,128)(2,1)} fusion(bf16[8,1024,640]{2,1,0:T(8,128)(2,1)} %fusion.29, bf16[1,1280,640]{2,1,0:T(8,128)(2,1)S(1)} %copy-done.8), kind=kOutput, calls=%fused_computation.47 | convolution fusion | flops 13432258560 | bytes 33095680 | tf_op jit(solution)/shard_map/bsf,df->bsd/dot_general | solution.py:37
  140.8 0.0 all-reduce.9.cloned.1.call-update
  140.8 0.0 copy-start.9
  140.8 0.0 all-reduce.7.cloned.1.call-start
  140.9 424.8 %all-reduce.5.cloned.1.call-done = f32[8,1024,1280]{2,1,0:T(8,128)} async-done(((f32[8,1024,1280]{2,1,0:T(8,128)}), f32[8,1024,1280]{2,1,0:T(8,128)}) %all-reduce.5.cloned.1.call-update) | async-done | bytes 41943056 | tf_op jit(solution)/shard_map/psum | solution.py:84
  565.6 41.8 %multiply_reduce_fusion.2 = (f32[8,1024]{1,0:T(8,128)S(1)}, f32[8,1024,1280]{2,1,0:T(8,128)}) fusion(f32[8,1024,1280]{2,1,0:T(8,128)} %param.9, f32[8,1024,1280]{2,1,0:T(8,128)} %all-reduce.5.cloned.1.call-done), kind=kLoop, calls=%fused_computation.19 | loop fusion | flops 31449088 | bytes 125861888 | tf_op jit(solution)/shard_map/reduce_sum | solution.py:11
  607.5 0.0 copy-start.6
  607.5 0.0 copy-done.9
  607.5 19.7 fusion.53
  627.2 29.4 %fusion.100 = (f32[8,2,1024]{2,1,0:T(2,128)S(1)}, f32[8,2,1024,1024]{2,3,1,0:T(8,128)}) fusion(bf16[8,1024,2,3,80]{1,4,3,2,0:T(8,128)(2,1)} %fusion.53), kind=kOutput, calls=%fused_computation.97 | convolution fusion | flops 2734687232 | bytes 72417280 | tf_op jit(solution)/shard_map/sub | solution.py:50
  656.5 0.0 copy-start.5
  656.5 24.4 %fusion.73 = bf16[8,2,80,1024]{3,2,1,0:T(8,128)(2,1)} fusion(bf16[8,1024,2,3,80]{1,4,3,2,0:T(8,128)(2,1)} %fusion.53, f32[8,2,1024,1024]{2,3,1,0:T(8,128)} %get-tuple-element.13, f32[8,2,1024]{2,1,0:T(2,128)S(1)} %get-tuple-element.12), kind=kOutput, calls=%fused_computation.76 | convolution fusion | flops 2719219712 | bytes 72417280 | tf_op jit(solution)/shard_map/bhqk,bkhe->bqhe/dot_general | solution.py:52
  680.9 19.7 convolution_bitcast_fusion
  700.6 0.0 all-reduce.7.cloned.1.call-update
  700.7 0.0 all-reduce.11.cloned.1.call-start
  700.7 124.2 %all-reduce.9.cloned.1.call-done = bf16[8,1024,1280]{2,1,0:T(8,128)(2,1)} async-done(((bf16[8,1024,1280]{2,1,0:T(8,128)(2,1)}), bf16[8,1024,1280]{2,1,0:T(8,128)(2,1)}) %all-reduce.9.cloned.1.call-update) | async-done | bytes 20971536 | tf_op jit(solution)/shard_map/psum | solution.py:86
  824.9 0.0 copy-done.3
  824.9 21.1 %fusion.6 = f32[8,1024]{1,0:T(8,128)S(1)} fusion(bf16[8,1024,1280]{2,1,0:T(8,128)(2,1)} %all-reduce.9.cloned.1.call-done, f32[8,1024,1280]{2,1,0:T(8,128)} %param.8, f32[8,1024]{1,0:T(8,128)S(1)} %copy-done.3), kind=kLoop, calls=%fused_computation.12 | loop fusion | flops 41934848 | bytes 62980096 | tf_op jit(solution)/shard_map/reduce_sum | solution.py:17
  846.1 463.2 %all-reduce.7.cloned.1.call-done = f32[8,1024,1280]{2,1,0:T(8,128)} async-done(((f32[8,1024,1280]{2,1,0:T(8,128)}), f32[8,1024,1280]{2,1,0:T(8,128)}) %all-reduce.7.cloned.1.call-update) | async-done | bytes 41943056 | tf_op jit(solution)/shard_map/psum | solution.py:89
  1309.2 73.7 %fusion.8 = (f32[8,1024,1280]{2,1,0:T(8,128)}, f32[8,1024,1280]{2,1,0:T(8,128)}) fusion(f32[8,1024,1280]{2,1,0:T(8,128)} %param.10, bf16[8,1024,1280]{2,1,0:T(8,128)(2,1)} %all-reduce.9.cloned.1.call-done, f32[8,1024,1280]{2,1,0:T(8,128)} %param.8, f32[8,1024]{1,0:T(8,128)S(1)} %broadcast_multiply_fusion.1, f32[8,1024]{1,0:T(8,128)S(1)} %copy-done.3, ...), kind=kLoop, calls=%fused_computation.14 | loop fusion | flops 73400320 | bytes 230752256 | tf_op jit(solution)/shard_map/add | solution.py:87
  1382.9 18.4 fusion.78
  1401.3 25.4 %convert_bitcast_fusion = bf16[8,1024,2,1,80]{1,4,2,0,3:T(8,128)(2,1)} fusion(bf16[8,1024,2,80]{1,3,2,0:T(8,128)(2,1)} %fusion.78, f32[8,2,1024,1024]{2,3,1,0:T(8,128)} %get-tuple-element.13, f32[8,2,1024]{2,1,0:T(2,128)S(1)} %get-tuple-element.12), kind=kOutput, calls=%fused_computation.71 | convolution fusion | flops 2719219712 | bytes 72417280 | tf_op jit(solution)/shard_map/bhqk,bqhe->bkhe/dot_general | solution.py:64
  1426.7 25.5 %fusion.72 = f32[8,2,1024,1024]{2,3,1,0:T(8,128)} fusion(bf16[8,1024,2,80]{1,3,2,0:T(8,128)(2,1)} %fusion.78, bf16[8,1024,2,3,80]{1,4,3,2,0:T(8,128)(2,1)} %fusion.53), kind=kOutput, calls=%fused_computation.75 | convolution fusion | flops 2684354560 | bytes 72351744 | tf_op jit(solution)/shard_map/bqhe,bkhe->bhqk/dot_general | solution.py:63
  1452.3 83.2 %convert_bitcast_fusion.2 = bf16[8,1024,2,1,80]{1,4,2,0,3:T(8,128)(2,1)} fusion(f32[8,2,1024,1024]{2,3,1,0:T(8,128)} %fusion.72, bf16[8,1024,2,3,80]{1,4,3,2,0:T(8,128)(2,1)} %fusion.53, f32[8,2,1024,1024]{2,3,1,0:T(8,128)} %get-tuple-element.13, f32[8,2,1024]{2,1,0:T(2,128)S(1)} %get-tuple-element.12), kind=kOutput, calls=%fused_computation.73 | convolution fusion | flops 2803123200 | bytes 273809408 | tf_op jit(solution)/shard_map/bhqk,bkhe->bqhe/dot_general | solution.py:66
  1535.5 83.8 %convert_bitcast_fusion.1 = bf16[8,1024,2,1,80]{1,4,2,0,3:T(8,128)(2,1)} fusion(f32[8,2,1024,1024]{2,3,1,0:T(8,128)} %fusion.72, bf16[8,1024,2,3,80]{1,4,3,2,0:T(8,128)(2,1)} %fusion.53, f32[8,2,1024,1024]{2,3,1,0:T(8,128)} %get-tuple-element.13, f32[8,2,1024]{2,1,0:T(2,128)S(1)} %get-tuple-element.12), kind=kOutput, calls=%fused_computation.72 | convolution fusion | flops 2803123200 | bytes 273809408 | tf_op jit(solution)/shard_map/bhqk,bqhe->bkhe/dot_general | solution.py:67
  1619.3 0.0 copy-done.10
  1619.3 21.1 %bitcast_convert_fusion = bf16[8,1024,1280]{2,1,0:T(8,128)(2,1)} fusion(bf16[8,1024,2,1,80]{1,4,2,0,3:T(8,128)(2,1)} %convert_bitcast_fusion, bf16[8,1024,2,1,80]{1,4,2,0,3:T(8,128)(2,1)} %convert_bitcast_fusion.1, bf16[8,1024,2,1,80]{1,4,2,0,3:T(8,128)(2,1)} %convert_bitcast_fusion.2, bf16[1,1280,2,3,80]{1,4,3,2,0:T(8,128)(2,1)S(1)} %copy-done.10), kind=kOutput, calls=%fused_computation.18 | convolution fusion | flops 10084679680 | bytes 30064640 | tf_op jit(solution)/shard_map/bshje,dhje->bsd/dot_general | solution.py:70
  1640.4 0.0 all-reduce.11.cloned.1.call-update
  1640.4 0.0 copy-start.4
  1640.4 27.0 %fusion.57 = f32[1,640,1280]{2,1,0:T(8,128)} fusion(f32[8,1024,1280]{2,1,0:T(8,128)} %param.11, f32[8,1024,640]{2,1,0:T(8,128)} %fusion.51), kind=kOutput, calls=%fused_computation.64 | convolution fusion | flops 13479444480 | bytes 66191360 | tf_op jit(solution)/shard_map/bsf,bsd->fd/dot_general | solution.py:33
  1667.4 0.0 copy-done.4
  1667.4 26.2 %fusion.56 = f32[1,1280,640]{2,1,0:T(8,128)} fusion(bf16[8,1024,640]{2,1,0:T(8,128)(2,1)} %fusion.29, f32[8,1024,1280]{2,1,0:T(8,128)} %param.8, f32[8,1024]{1,0:T(8,128)S(1)} %copy-done.4), kind=kOutput, calls=%fused_computation.63 | convolution fusion | flops 13442744320 | bytes 55738368 | tf_op jit(solution)/shard_map/bsd,bsf->df/dot_general | solution.py:36
  1693.6 17.0 fusion.67
  1710.6 20.1 %fusion.60 = f32[1,1280,2,3,80]{1,4,3,2,0:T(8,128)} fusion(f32[8,1024,1280]{2,1,0:T(8,128)} %get-tuple-element.9, f32[8,1024]{1,0:T(8,128)S(1)} %copy-done.7, bf16[8,1024,2,1,80]{1,4,2,0,3:T(8,128)(2,1)} %convert_bitcast_fusion, bf16[8,1024,2,1,80]{1,4,2,0,3:T(8,128)(2,1)} %convert_bitcast_fusion.1, bf16[8,1024,2,1,80]{1,4,2,0,3:T(8,128)(2,1)} %convert_bitcast_fusion.2), kind=kOutput, calls=%fused_computation.65 | convolution fusion | flops 10095165440 | bytes 52297728 | tf_op jit(solution)/shard_map/bsd,bshje->dhje/dot_general | solution.py:69
  1730.7 164.7 %all-reduce.11.cloned.1.call-done = bf16[8,1024,1280]{2,1,0:T(8,128)(2,1)} async-done(((bf16[8,1024,1280]{2,1,0:T(8,128)(2,1)}), bf16[8,1024,1280]{2,1,0:T(8,128)(2,1)}) %all-reduce.11.cloned.1.call-update) | async-done | bytes 20971536 | tf_op jit(solution)/shard_map/psum | solution.py:91
  1895.5 20.7 %fusion.9 = f32[8,1024]{1,0:T(8,128)S(1)} fusion(bf16[8,1024,1280]{2,1,0:T(8,128)(2,1)} %all-reduce.11.cloned.1.call-done, f32[8,1024,1280]{2,1,0:T(8,128)} %get-tuple-element.9, f32[8,1024]{1,0:T(8,128)S(1)} %copy-done.7), kind=kLoop, calls=%fused_computation.15 | loop fusion | flops 41934848 | bytes 62980096 | tf_op jit(solution)/shard_map/reduce_sum | solution.py:17
  1916.2 0.0 copy-start.1
  1916.2 47.3 %fusion.11 = f32[8,1024,1280]{2,1,0:T(8,128)} fusion(f32[8,1024,1280]{2,1,0:T(8,128)} %param.11, bf16[8,1024,1280]{2,1,0:T(8,128)(2,1)} %all-reduce.11.cloned.1.call-done, f32[8,1024,1280]{2,1,0:T(8,128)} %get-tuple-element.9, f32[8,1024]{1,0:T(8,128)S(1)} %broadcast_multiply_fusion, f32[8,1024]{1,0:T(8,128)S(1)} %copy-done.7), kind=kLoop, calls=%fused_computation.17 | loop fusion | flops 62914560 | bytes 146866176 | tf_op jit(solution)/shard_map/add | solution.py:92
  (14 shorter events, 0.1 us)
Async XLA Ops:
  7.2 45.0 %copy-start = (bf16[1,640,1280]{2,1,0:T(8,128)(2,1)S(1)}, bf16[1,640,1280]{2,1,0:T(8,128)(2,1)}, u32[]{:S(2)}) copy-start(bf16[1,640,1280]{2,1,0:T(8,128)(2,1)} %param.15) | copy-start | bytes 4915204
  7.2 16.7 copy-start.8
  7.2 558.4 %all-reduce.5.cloned.1.call-start = ((), (), s32[]{:S(2)}) async-start(), calls=%async_computation | async-start | bytes 83886080 | tf_op jit(solution)/shard_map/psum | solution.py:84
  23.8 28.3 %copy-start.2 = (f32[8,1024]{1,0:T(8,128)}, f32[8,1024]{1,0:T(8,128)S(1)}, u32[]{:S(2)}) copy-start(f32[8,1024]{1,0:T(8,128)S(1)} %add_rsqrt_fusion.1) | copy-start | bytes 98308
  82.7 742.2 %all-reduce.9.cloned.1.call-start = ((), (), s32[]{:S(2)}) async-start(), calls=%async_computation.2 | async-start | bytes 41943040 | tf_op jit(solution)/shard_map/psum | solution.py:86
  140.8 466.7 %copy-start.9 = (bf16[1,1280,2,3,80]{1,4,3,2,0:T(8,128)(2,1)S(1)}, bf16[1,1280,2,3,80]{1,4,3,2,0:T(8,128)(2,1)}, u32[]{:S(2)}) copy-start(bf16[1,1280,2,3,80]{1,4,3,2,0:T(8,128)(2,1)} %param.12) | copy-start | bytes 3686404
  140.8 1168.4 %all-reduce.7.cloned.1.call-start = ((), (), s32[]{:S(2)}) async-start(), calls=%async_computation.1 | async-start | bytes 83886080 | tf_op jit(solution)/shard_map/psum | solution.py:89
  607.5 19.7 copy-start.6
  656.5 24.4 %copy-start.5 = (bf16[1,2,80,1280]{3,2,1,0:T(8,128)(2,1)S(1)}, bf16[1,2,80,1280]{3,2,1,0:T(8,128)(2,1)}, u32[]{:S(2)}) copy-start(bf16[1,2,80,1280]{3,2,1,0:T(8,128)(2,1)} %param.13) | copy-start | bytes 1228804
  700.6 124.3 %copy-start.3 = (f32[8,1024]{1,0:T(8,128)S(1)}, f32[8,1024]{1,0:T(8,128)}, u32[]{:S(2)}) copy-start(f32[8,1024]{1,0:T(8,128)} %copy-done.2) | copy-start | bytes 98308
  700.7 1194.8 %all-reduce.11.cloned.1.call-start = ((), (), s32[]{:S(2)}) async-start(), calls=%async_computation.3 | async-start | bytes 41943040 | tf_op jit(solution)/shard_map/psum | solution.py:91
  1535.5 83.8 %copy-start.10 = (bf16[1,1280,2,3,80]{1,4,3,2,0:T(8,128)(2,1)S(1)}, bf16[1,1280,2,3,80]{1,4,3,2,0:T(8,128)(2,1)}, u32[]{:S(2)}) copy-start(bf16[1,1280,2,3,80]{1,4,3,2,0:T(8,128)(2,1)} %param.12) | copy-start | bytes 3686404
  1640.4 27.0 %copy-start.4 = (f32[8,1024]{1,0:T(8,128)S(1)}, f32[8,1024]{1,0:T(8,128)}, u32[]{:S(2)}) copy-start(f32[8,1024]{1,0:T(8,128)} %copy-done.2) | copy-start | bytes 98308
  1693.6 17.0 copy-start.7
  1916.2 47.3 %copy-start.1 = (bf16[1,640,1280]{2,1,0:T(8,128)(2,1)S(1)}, bf16[1,640,1280]{2,1,0:T(8,128)(2,1)}, u32[]{:S(2)}) copy-start(bf16[1,640,1280]{2,1,0:T(8,128)(2,1)} %param.15) | copy-start | bytes 4915204
Sparse Core Ops, SparseCore 0:
  82.8 482.7 all-reduce.4
  569.9 254.9 all-reduce.8
  829.2 479.9 all-reduce.6
  1640.5 254.9 all-reduce.10
where the time goes:
time: 1980 us; the launch traced here: 1970 us
  waiting for transfers between devices  1180 us (60%)
  matrix products  558 us (28%)
  other arithmetic  221 us (11%)
    psum x1, waiting for transfers between devices, local_backward(): run_y1 = run_y1 - lax.psum(f_part, 'tp')  463 us
    psum x1, waiting for transfers between devices, local_backward(): low_x2 = run_y2 - lax.psum(g_part, 'tp')  425 us
    psum x1, waiting for transfers between devices, local_backward(): grad_n = lax.psum(fn_part.astype(jnp.bfloat16), 'tp').astype(jnp.float32)  165 us
    psum x1, waiting for transfers between devices, local_backward(): grad_n = lax.psum(gn_part.astype(jnp.bfloat16), 'tp').astype(jnp.float32)  124 us
    dot_general x1, matrix products, attn_backward(): jnp.einsum('bhqk,bqhe->bkhe', grad_s, q_rows, preferred_element_type=jnp....  83.8 us
    dot_general x1, matrix products, attn_backward(): jnp.einsum('bhqk,bkhe->bqhe', grad_s, k_rows, preferred_element_type=jnp....  83.2 us
    add x1, other arithmetic, local_backward(): run_c1 = run_c1 + rms_back(g_norm, grad_n)  73.7 us
    reduce_sum x2, other arithmetic, rms_fwd(): jnp.mean(x_in * x_in, axis=-1, keepdims=True) + NORM_EPS  58.4 us
  transfers between devices with their start and end apart: 4, of which 4 were waited for; matrix products, arithmetic and copies ran while one was open for 15% of the time, Pallas kernels for 0%

commit v1 on v0

v1 whole, which is shorter than its diff:
```python
import functools
import math

import jax
import jax.numpy as jnp
from jax import lax
from jax.experimental import pallas as pl
from jax.experimental.pallas import tpu as pltpu
from jax.sharding import PartitionSpec as P

F32, BF16 = jnp.float32, jnp.bfloat16
NORM_EPS = 1e-6
GELU_C = math.sqrt(2.0 / math.pi)
GELU_K = 0.044715
D = 1280
SEQ = 1024
HEAD = 80
HEADS_DEV = 2
QKV = 3 * HEAD * HEADS_DEV
OUT = HEAD * HEADS_DEV
FFD = 640
ROWS = 512
STEPS = 4
SCALE = 1.0 / math.sqrt(HEAD)
VMEM_CAP = 62 * 1024 * 1024


def dot(a, b, dims=((1,), (0,))):
    return lax.dot_general(a, b, (dims, ((), ())), preferred_element_type=F32)


NT = ((1,), (1,))
TN = ((0,), (0,))


def inv_rms(x):
    return lax.rsqrt(jnp.mean(x * x, axis=-1, keepdims=True) + NORM_EPS)


def gelu_pair(h):
    sq = h * h
    t = jnp.tanh(h * (GELU_C + (GELU_C * GELU_K) * sq))
    cdf = 0.5 + 0.5 * t
    act = h * cdf
    slope = cdf + (0.5 * h) * (1.0 - t * t) * (GELU_C + (3.0 * GELU_C * GELU_K) * sq)
    return act.astype(BF16), slope


def cost(flops, nbytes):
    return pl.CostEstimate(flops=int(flops), bytes_accessed=int(nbytes), transcendentals=0)


def any_spec():
    return pl.BlockSpec(memory_space=pl.ANY)


def params(**kw):
    return pltpu.CompilerParams(vmem_limit_bytes=VMEM_CAP, **kw)


def mlp_own_kernel(base, y1, c2, w1o, w1p, w2o, w2p, n_out, cot_out, act_out, dh_out, gp_out, np_out, w1, w2, sems):
    @pl.when(pl.program_id(0) == 0)
    def _():
        cps = [
            pltpu.make_async_copy(w1o, w1.at[:, pl.ds(0, FFD)], sems.at[0]),
            pltpu.make_async_copy(w1p, w1.at[:, pl.ds(FFD, FFD)], sems.at[1]),
            pltpu.make_async_copy(w2o, w2.at[pl.ds(0, FFD), :], sems.at[2]),
            pltpu.make_async_copy(w2p, w2.at[pl.ds(FFD, FFD), :], sems.at[3]),
        ]
        for cp in cps:
            cp.start()
        for cp in cps:
            cp.wait()

    y = y1[...]
    n_out[...] = (y * inv_rms(y)).astype(BF16)
    cot_out[...] = c2[...].astype(BF16)
    act, slope = gelu_pair(dot(n_out[...], w1[...]))
    act_out[...] = act
    dh = (dot(cot_out[...], w2[...], NT) * slope).astype(BF16)
    dh_out[...] = dh
    gp_out[...] = dot(act, w2[...])
    np_out[...] = dot(dh, w1[...], NT)


def mlp_own(core, y1, c2, w1o, w1p, w2o, w2p):
    half = STEPS * SEQ
    blocks = half // ROWS
    row_in = pl.BlockSpec((ROWS, D), lambda i, base: (base[0] * blocks + i, 0))
    row_out = pl.BlockSpec((ROWS, D), lambda i, base: (i, 0))
    return pl.pallas_call(
        mlp_own_kernel,
        name="mlp_own",
        grid_spec=pltpu.PrefetchScalarGridSpec(
            num_scalar_prefetch=1,
            grid=(blocks,),
            in_specs=[row_in, row_in] + [any_spec()] * 4,
            out_specs=[row_out] * 6,
            scratch_shapes=[
                pltpu.VMEM((D, 2 * FFD), BF16),
                pltpu.VMEM((2 * FFD, D), BF16),
                pltpu.SemaphoreType.DMA((4,)),
            ],
        ),
        out_shape=[jax.ShapeDtypeStruct((half, D), BF16)] * 4 + [jax.ShapeDtypeStruct((half, D), F32)] * 2,
        compiler_params=params(dimension_semantics=("arbitrary",)),
        cost_estimate=cost(4 * 2 * half * D * 2 * FFD, 120e6),
    )(core, y1, c2, w1o, w1p, w2o, w2p)


def grad_kernel(split_rows, a, b, dep, own, peer, acc, sems):
    i = pl.program_id(0)

    @pl.when(i == 0)
    def _():
        acc[...] = jnp.zeros_like(acc)

    acc[...] += dot(a[...], b[...], TN)

    @pl.when(i == pl.num_programs(0) - 1)
    def _():
        part = lambda k: acc.at[pl.ds(k * FFD, FFD), :] if split_rows else acc.at[:, pl.ds(k * FFD, FFD)]
        cps = [pltpu.make_async_copy(part(0), own, sems.at[0]), pltpu.make_async_copy(part(1), peer, sems.at[1])]
        for cp in cps:
            cp.start()
        for cp in cps:
            cp.wait()


def mlp_grad(split_rows, a, b, dep):
    half = STEPS * SEQ
    row = pl.BlockSpec((ROWS, D), lambda i: (i, 0))
    shape = (FFD, D) if split_rows else (D, FFD)
    return pl.pallas_call(
        functools.partial(grad_kernel, split_rows),
        name="mlp_grad",
        grid=(half // ROWS,),
        in_specs=[row, row, any_spec()],
        out_specs=[any_spec()] * 2,
        scratch_shapes=[pltpu.VMEM((D, 2 * FFD), F32), pltpu.SemaphoreType.DMA((2,))],
        out_shape=[jax.ShapeDtypeStruct(shape, F32)] * 2,
        compiler_params=params(dimension_semantics=("arbitrary",)),
        cost_estimate=cost(2 * half * D * 2 * FFD, 30e6),
    )(a, b, dep)


def mlp_rest_kernel(step, base, n_in, cot_in, y1, y2, c1, gp, np_, *refs):
    ws = refs[:12]
    x2_out, d1_out = refs[13:15]
    w1, w2, late, accg, accn, wsem, lsem, osem = refs[15:]
    i = pl.program_id(0)
    row = base[0] * (STEPS * SEQ) + step * SEQ + i * ROWS
    row = pl.multiple_of(row, ROWS)
    loc = pl.multiple_of(step * SEQ + i * ROWS, ROWS)
    out_row = pl.multiple_of(i * ROWS, ROWS)

    def w_copies(k):
        a1o, a1p, a2o, a2p = ws[4 * k : 4 * k + 4]
        return [
            pltpu.make_async_copy(a1o, w1.at[k, :, pl.ds(0, FFD)], wsem.at[k, 0]),
            pltpu.make_async_copy(a1p, w1.at[k, :, pl.ds(FFD, FFD)], wsem.at[k, 1]),
            pltpu.make_async_copy(a2o, w2.at[k, pl.ds(0, FFD), :], wsem.at[k, 2]),
            pltpu.make_async_copy(a2p, w2.at[k, pl.ds(FFD, FFD), :], wsem.at[k, 3]),
        ]

    late_copies = [
        pltpu.make_async_copy(src.at[pl.ds(at, ROWS), :], late.at[j], lsem.at[j])
        for j, (src, at) in enumerate(((gp, loc), (np_, loc), (y2, row), (c1, row), (y1, row)))
    ]
    outs = [
        pltpu.make_async_copy(accg, x2_out.at[pl.ds(out_row, ROWS), :], osem.at[0]),
        pltpu.make_async_copy(accn, d1_out.at[pl.ds(out_row, ROWS), :], osem.at[1]),
    ]

    @pl.when(i == 0)
    def _():
        for k in range(3):
            for cp in w_copies(k):
                cp.start()

    for cp in late_copies:
        cp.start()

    @pl.when(i > 0)
    def _():
        for cp in outs:
            cp.wait()

    def chunk(k):
        @pl.when(i == 0)
        def _():
            for kk in range(3):
                @pl.when(k == kk)
                def _():
                    for cp in w_copies(kk):
                        cp.wait()

        act, slope = gelu_pair(dot(n_in[...], w1[k]))
        dh = (dot(cot_in[...], w2[k], NT) * slope).astype(BF16)
        g = dot(act, w2[k])
        gn = dot(dh, w1[k], NT)
        return g, gn

    def body(k, _):
        g, gn = chunk(k)

        @pl.when(k == 0)
        def _():
            accg[...] = g
            accn[...] = gn

        @pl.when(k == 1)
        def _():
            accg[...] += g
            accn[...] += gn

        @pl.when(k == 2)
        def _():
            for cp in late_copies:
                cp.wait()
            late[0] = late[0] + g
            late[1] = late[1] + gn

        return 0

    lax.fori_loop(0, 3, body, 0)

    def finish(r, _):
        at = pl.ds(pl.multiple_of(r * 8, 8), 8)
        accg[at, :] = late[2, at, :] - (accg[at, :] + late[0, at, :])
        y = late[4, at, :]
        k = inv_rms(y)
        nf = y * k
        gn = accn[at, :] + late[1, at, :]
        accn[at, :] = late[3, at, :] + k * (gn - nf * jnp.mean(nf * gn, axis=-1, keepdims=True))
        return 0

    lax.fori_loop(0, ROWS // 8, finish, 0, unroll=8)
    for cp in outs:
        cp.start()

    @pl.when(i == pl.num_programs(0) - 1)
    def _():
        for cp in outs:
            cp.wait()


def mlp_rest(step, core, n_in, cot_in, y1, y2, c1, gp, np_, ws, dep):
    blocks = SEQ // ROWS
    row_in = pl.BlockSpec((ROWS, D), lambda i, base: (step * blocks + i, 0))
    return pl.pallas_call(
        functools.partial(mlp_rest_kernel, step),
        name="mlp_rest",
        grid_spec=pltpu.PrefetchScalarGridSpec(
            num_scalar_prefetch=1,
            grid=(blocks,),
            in_specs=[row_in, row_in] + [any_spec()] * 18,
            out_specs=[any_spec()] * 2,
            scratch_shapes=[
                pltpu.VMEM((3, D, 2 * FFD), BF16),
                pltpu.VMEM((3, 2 * FFD, D), BF16),
                pltpu.VMEM((5, ROWS, D), F32),
                pltpu.VMEM((ROWS, D), F32),
                pltpu.VMEM((ROWS, D), F32),
                pltpu.SemaphoreType.DMA((3, 4)),
                pltpu.SemaphoreType.DMA((5,)),
                pltpu.SemaphoreType.DMA((2,)),
            ],
        ),
        out_shape=[jax.ShapeDtypeStruct((SEQ, D), F32)] * 2,
        compiler_params=params(dimension_semantics=("arbitrary",)),
        cost_estimate=cost(12 * 2 * SEQ * D * 2 * FFD, 60e6),
    )(core, n_in, cot_in, y1, y2, c1, gp, np_, *ws, dep)


def attn_kernel(step, chained, base, x2o, x2p, d1o, d1p, wq, wo, *refs):
    refs = refs[5:] if chained else refs[1:]
    x2_out, d1_out, aq, ao, oT_out, fn_out = refs[:6]
    (xb, cb, n2, cot, qkvT, dqkvT, dOT, oT, kb, vb, dk, dv, fnb, accq, acco, isem, wsem, osem, asem) = refs[6:]
    i = pl.program_id(0)
    core = base[0]

    def in_copies(j):
        sx, sc = ((x2o, d1o), (x2p, d1p))[j]
        return [
            pltpu.make_async_copy(sx, xb.at[j], isem.at[j, 0]),
            pltpu.make_async_copy(sc, cb.at[j], isem.at[j, 1]),
        ]

    def out_copies(j):
        owner = core if j == 0 else 1 - core
        row = pl.multiple_of(owner * (STEPS * SEQ) + step * SEQ, SEQ)
        return [
            pltpu.make_async_copy(xb.at[j], x2_out.at[pl.ds(row, SEQ), :], wsem.at[j, 0]),
            pltpu.make_async_copy(cb.at[j], d1_out.at[pl.ds(row, SEQ), :], wsem.at[j, 1]),
        ]

    def res_copies(j):
        owner = core if j == 0 else 1 - core
        col = pl.multiple_of(owner * SEQ, SEQ)
        return [
            pltpu.make_async_copy(oT, oT_out.at[:, pl.ds(col, SEQ)], osem.at[0]),
            pltpu.make_async_copy(fnb, fn_out.at[owner], osem.at[1]),
        ]

    @pl.when(i == 0)
    def _():
        for j in range(2):
            for cp in in_copies(j):
                cp.start()
        if chained:
            cps = [pltpu.make_async_copy(aq, accq, asem.at[0]), pltpu.make_async_copy(ao, acco, asem.at[1])]
            for cp in cps:
                cp.start()
            for cp in cps:
                cp.wait()
        else:
            accq[...] = jnp.zeros_like(accq)
            acco[...] = jnp.zeros_like(acco)

    for j in range(2):
        @pl.when(i == j)
        def _():
            for cp in in_copies(j):
                cp.wait()
            for cp in out_copies(j):
                cp.start()

    x = xb[i]
    n2[...] = (x * inv_rms(x)).astype(BF16)
    cot[...] = cb[i].astype(BF16)
    qkvT[...] = dot(wq[...], n2[...], NT).astype(BF16)
    dO = dot(cot[...], wo[...], NT).astype(BF16)
    dOT[...] = dO.T

    @pl.when(i == 1)
    def _():
        for cp in res_copies(0):
            cp.wait()

    def head(h, _):
        at = pl.multiple_of(h * (3 * HEAD), 16)
        oat = pl.multiple_of(h * HEAD, 16)
        kT = qkvT[pl.ds(at + HEAD, HEAD), :]
        vT = qkvT[pl.ds(at + 2 * HEAD, HEAD), :]
        kb[...] = kT.T
        vb[...] = vT.T
        for qb in range(SEQ // ROWS):
            cols = pl.ds(qb * ROWS, ROWS)
            qT = qkvT[pl.ds(at, HEAD), cols]
            gT = dOT[pl.ds(oat, HEAD), cols]
            s = dot(kb[...], qT)
            m = jnp.max(s, axis=0, keepdims=True)
            p = jnp.exp2((s - m) * (SCALE * math.log2(math.e)))
            p = p * (1.0 / jnp.sum(p, axis=0, keepdims=True))
            pb = p.astype(BF16)
            dp = dot(vb[...], gT)
            r = jnp.sum(dp * p, axis=0, keepdims=True)
            ds = (p * (dp - r) * SCALE).astype(BF16)
            oT[pl.ds(oat, HEAD), cols] = dot(qkvT[pl.ds(at + 2 * HEAD, HEAD), :], pb).astype(BF16)
            dvp = dot(pb, gT.T)
            dqkvT[pl.ds(at, HEAD), cols] = dot(qkvT[pl.ds(at + HEAD, HEAD), :], ds).astype(BF16)
            dkp = dot(ds, qT.T)
            if qb == 0:
                dv[...] = dvp
                dk[...] = dkp
            else:
                dqkvT[pl.ds(at + 2 * HEAD, HEAD), :] = (dv[...] + dvp).astype(BF16).T
                dqkvT[pl.ds(at + HEAD, HEAD), :] = (dk[...] + dkp).astype(BF16).T
        return 0

    lax.fori_loop(0, HEADS_DEV, head, 0)
    fnb[...] = dot(dqkvT[...], wq[...], TN).astype(BF16)
    for j in range(2):
        @pl.when(i == j)
        def _():
            for cp in res_copies(j):
                cp.start()
    accq[...] += dot(dqkvT[...], n2[...])
    acco[...] += dot(oT[...], cot[...])

    @pl.when(i == 1)
    def _():
        cps = [pltpu.make_async_copy(accq, aq, asem.at[0]), pltpu.make_async_copy(acco, ao, asem.at[1])]
        for cp in cps:
            cp.start()
        for cp in cps + res_copies(1) + out_copies(0) + out_copies(1):
            cp.wait()


def attn(step, core, x2o, x2p, d1o, d1p, wq, wo, dep, chain):
    full = jax.ShapeDtypeStruct((2 * STEPS * SEQ, D), F32)
    whole = lambda shape: pl.BlockSpec(shape, lambda i, base: (0, 0))
    chained = chain is not None
    ins = [core, x2o, x2p, d1o, d1p, wq, wo, dep] + (list(chain) if chained else [])
    return pl.pallas_call(
        functools.partial(attn_kernel, step, chained),
        name="attn",
        grid_spec=pltpu.PrefetchScalarGridSpec(
            num_scalar_prefetch=1,
            grid=(2,),
            in_specs=[any_spec()] * 4 + [whole((QKV, D)), whole((OUT, D))] + [any_spec()] * (5 if chained else 1),
            out_specs=[any_spec()] * 6,
            scratch_shapes=[
                pltpu.VMEM((2, SEQ, D), F32),
                pltpu.VMEM((2, SEQ, D), F32),
                pltpu.VMEM((SEQ, D), BF16),
                pltpu.VMEM((SEQ, D), BF16),
                pltpu.VMEM((QKV, SEQ), BF16),
                pltpu.VMEM((QKV, SEQ), BF16),
                pltpu.VMEM((OUT, SEQ), BF16),
                pltpu.VMEM((OUT, SEQ), BF16),
                pltpu.VMEM((SEQ, HEAD), BF16),
                pltpu.VMEM((SEQ, HEAD), BF16),
                pltpu.VMEM((SEQ, HEAD), F32),
                pltpu.VMEM((SEQ, HEAD), F32),
                pltpu.VMEM((SEQ, D), BF16),
                pltpu.VMEM((QKV, D), F32),
                pltpu.VMEM((OUT, D), F32),
                pltpu.SemaphoreType.DMA((2, 2)),
                pltpu.SemaphoreType.DMA((2, 2)),
                pltpu.SemaphoreType.DMA((2,)),
                pltpu.SemaphoreType.DMA((2,)),
            ],
        ),
        out_shape=[
            full,
            full,
            jax.ShapeDtypeStruct((QKV, D), F32),
            jax.ShapeDtypeStruct((OUT, D), F32),
            jax.ShapeDtypeStruct((OUT, 2 * SEQ), BF16),
            jax.ShapeDtypeStruct((2, SEQ, D), BF16),
        ],
        input_output_aliases={8 + k: k for k in range(4)} if chained else {},
        compiler_params=params(dimension_semantics=("arbitrary",)),
        cost_estimate=cost(24e9, 60e6),
    )(*ins)


def out_proj_kernel(y1, oT, wo, *refs):
    refs[-1][...] = y1[...] - dot(oT[...], wo[...], TN)


def out_proj(step, y1, oT, wo, dep, chain):
    per = SEQ // ROWS
    chained = chain is not None
    row = pl.BlockSpec((ROWS, D), lambda i: ((i // per) * (STEPS * per) + step * per + i % per, 0))
    return pl.pallas_call(
        out_proj_kernel,
        name="out_proj",
        grid=(2 * per,),
        in_specs=[row, pl.BlockSpec((8 * OUT, ROWS), lambda i: (0, i)), pl.BlockSpec((8 * OUT, D), lambda i: (0, 0)), any_spec()]
        + [any_spec()] * (1 if chained else 0),
        out_specs=row,
        out_shape=jax.ShapeDtypeStruct((2 * STEPS * SEQ, D), F32),
        input_output_aliases={4: 0} if chained else {},
        compiler_params=params(dimension_semantics=("arbitrary",)),
        cost_estimate=cost(2 * 2 * SEQ * D * D, 30e6),
    )(y1, oT, wo, dep, *([chain] if chained else []))


def norm_back_kernel(per, base, x2o, x2p, f, c2, *refs):
    out = refs[-1]

    def run(x_ref):
        def rows(r, _):
            at = pl.ds(pl.multiple_of(r * 16, 16), 16)
            x = x_ref[at, :]
            k = inv_rms(x)
            nf = x * k
            g = f[at, :].astype(F32)
            out[at, :] = c2[at, :] + k * (g - nf * jnp.mean(nf * g, axis=-1, keepdims=True))
            return 0

        lax.fori_loop(0, ROWS // 16, rows, 0, unroll=4)

    @pl.when(pl.program_id(0) < per)
    def _():
        run(x2o)

    @pl.when(pl.program_id(0) >= per)
    def _():
        run(x2p)


def norm_back(step, core, x2o, x2p, f, c2, dep, chain):
    per = SEQ // ROWS
    chained = chain is not None
    own = pl.BlockSpec((ROWS, D), lambda i, base: (jnp.minimum(i, per - 1), 0))
    peer = pl.BlockSpec((ROWS, D), lambda i, base: (jnp.maximum(i - per, 0), 0))

    def at(i, base, stride, off):
        owner = jnp.where(i < per, base[0], 1 - base[0])
        return (owner * (stride * per) + off * per + i % per, 0)

    row = pl.BlockSpec((ROWS, D), lambda i, base: at(i, base, STEPS, step))
    frow = pl.BlockSpec((ROWS, D), lambda i, base: at(i, base, 1, 0))
    return pl.pallas_call(
        functools.partial(norm_back_kernel, per),
        name="norm_back",
        grid_spec=pltpu.PrefetchScalarGridSpec(
            num_scalar_prefetch=1,
            grid=(2 * per,),
            in_specs=[own, peer, frow, row, any_spec()] + [any_spec()] * (1 if chained else 0),
            out_specs=row,
        ),
        out_shape=jax.ShapeDtypeStruct((2 * STEPS * SEQ, D), F32),
        input_output_aliases={6: 0} if chained else {},
        compiler_params=params(dimension_semantics=("arbitrary",)),
        cost_estimate=cost(4e9, 40e6),
    )(core, x2o, x2p, f, c2, dep, *([chain] if chained else []))


def solution(mesh):
    act_spec = P("dp", None, None)
    weight_specs = (P(None, None, "tp", None, None), P(None, "tp", None, None), P(None, None, "tp"), P(None, "tp", None))
    grad_specs = (P("dp", None, "tp", None, None), P("dp", "tp", None, None), P("dp", None, "tp"), P("dp", "tp", None))

    pair_core = [(t, t ^ 1) for t in range(8)]
    pair_a = [(t, t ^ (4 if t & 1 else 2)) for t in range(8)]
    pair_b = [(t, t ^ (2 if t & 1 else 4)) for t in range(8)]

    def swap(x, pairs):
        return lax.ppermute(x, "tp", pairs)

    def local_backward(out_y1, out_y2, cot_y1, cot_y2, w_qkv, w_out, w_up, w_down):
        core = lax.axis_index("tp") & 1
        base = core.reshape(1).astype(jnp.int32)
        flat = lambda z: z.reshape(2 * STEPS * SEQ, D)
        y1, y2, c1, c2 = flat(out_y1), flat(out_y2), flat(cot_y1), flat(cot_y2)
        w1, w2 = w_up[0], w_down[0]
        wq = jnp.transpose(w_qkv[0], (1, 2, 3, 0)).reshape(QKV, D)
        wo = w_out[0].reshape(OUT, D)

        w1p, w2p = swap(w1, pair_core), swap(w2, pair_core)
        w1a, w2a = swap(w1, pair_a), swap(w2, pair_a)
        w1b, w2b = swap(w1, pair_b), swap(w2, pair_b)
        n_all, cot_all, act, dh, gp, np_ = mlp_own(base, y1, c2, w1, w1p, w2, w2p)
        w1a, w2a, w1b, w2b, np_ = lax.optimization_barrier((w1a, w2a, w1b, w2b, np_))
        w1d, w2d = swap(w1b, pair_a), swap(w2b, pair_a)
        d1o, d1p = mlp_grad(False, n_all, dh, np_)
        rest = []
        for u, d in ((w1a, w2a), (w1b, w2b)):
            rest += [u, swap(u, pair_core), d, swap(d, pair_core)]
        w1d, w2d, d1o = lax.optimization_barrier((w1d, w2d, d1o))
        rest += [w1d, swap(w1d, pair_core), w2d, swap(w2d, pair_core)]
        wo_all = lax.all_gather(wo, "tp", axis=0, tiled=True)

        x2s, d1s = [None] * STEPS, [None] * STEPS
        ots, fns = [None] * STEPS, [None] * STEPS
        chain = x1 = dx2 = None

        def mlp(s, dep):
            x, d = mlp_rest(s, base, n_all, cot_all, y1, y2, c1, gp, np_, rest, dep)
            x2s[s], d1s[s] = (x, swap(x, pair_core)), (d, swap(d, pair_core))
            return x

        def att(s, dep):
            nonlocal chain
            *chain, oT, fn = attn(s, base, *x2s[s], *d1s[s], wq, wo, dep, chain)
            ots[s] = lax.all_gather(oT, "tp", axis=0, tiled=True)
            if s:
                fn, fns[s - 1] = lax.optimization_barrier((fn, fns[s - 1]))
            fns[s] = lax.psum(fn.reshape(2 * SEQ, D), "tp")
            return chain[3]

        def proj(s, dep):
            nonlocal x1
            x1 = out_proj(s, y1, ots[s], wo_all, dep, x1)
            return x1

        def back(s, dep):
            nonlocal dx2
            dx2 = norm_back(s, base, *x2s[s], fns[s], c2, dep, dx2)
            return dx2

        t = mlp(0, d1o)
        d2o, d2p = mlp_grad(True, act, cot_all, t)
        g_up = d1o + swap(d1p, pair_core)
        g_down = d2o + swap(d2p, pair_core)
        t = att(0, d2o)
        t = mlp(1, t)
        t = proj(0, t)
        t = att(1, t)
        t = mlp(2, t)
        t = back(0, t)
        t = proj(1, t)
        t = att(2, t)
        t = mlp(3, t)
        t = back(1, t)
        t = proj(2, t)
        t = att(3, t)
        t = back(2, t)
        t = proj(3, t)
        back(3, t)

        x2, dx1, aq, ao = chain
        full = lambda z: z.reshape(2 * STEPS, SEQ, D)
        g_qkv = jnp.transpose(aq.reshape(HEADS_DEV, 3, HEAD, D), (3, 0, 1, 2))
        g_out = ao.reshape(HEADS_DEV, HEAD, D)
        return full(x1), full(x2), full(dx1), full(dx2), g_qkv[None], g_out[None], g_up[None], g_down[None]

    return jax.shard_map(
        local_backward,
        mesh=mesh,
        in_specs=(act_spec,) * 4 + weight_specs,
        out_specs=(act_spec,) * 4 + grad_specs,
        check_vma=False,
    )
```

time: 1980 us -> 838 us (0.42)
  waiting for transfers between devices: 1180 us -> 130 us
  Pallas kernels: 0 us -> 663 us
  matrix products: 558 us -> 0 us
  other arithmetic: 221 us -> 8.17 us
    psum x4, waiting for transfers between devices: 1180 us -> 89.1 us  [att(): fns[s] = lax.psum(fn.reshape(2 * SEQ, D), 'tp')]
    pallas_call x0 -> x19, Pallas kernels: none -> 663 us  [the longest x4 276 us: mlp_rest(): pl.pallas_call(functools.partial(mlp_rest_kernel, step), name='mlp_rest',...]
    dot_general x17 -> x0, matrix products: 528 us -> none  [the longest x1 83.8 us: attn_backward(): jnp.einsum('bhqk,bqhe->bkhe', grad_s, q_rows, preferred_element_type=jnp....]
    add x2 -> x0, other arithmetic: 121 us -> none  [the longest x1 73.7 us: local_backward(): run_c1 = run_c1 + rms_back(g_norm, grad_n)]
    reduce_sum x4 -> x0, other arithmetic: 100 us -> none  [the longest x2 58.4 us: rms_fwd(): jnp.mean(x_in * x_in, axis=-1, keepdims=True) + NORM_EPS]
    sub x1 -> x0, matrix products: 29.4 us -> none  [attn_forward(): attn_prob = jax.nn.softmax(scores, axis=-1)]
    ppermute x0 -> x24, waiting for transfers between devices: none -> 25.2 us  [swap(): return lax.ppermute(x, 'tp', pairs)]
  transfers between devices with their start and end apart: 4 -> 33, of which waited for: 4 -> 9; matrix products, arithmetic and copies ran while one was open for 15% -> 1% of each run, Pallas kernels for 0% -> 70%
where the time goes in v1:
time: 838 us; the launch traced here: 831 us
  Pallas kernels  663 us (79%)
  waiting for transfers between devices  130 us (16%)
  between operations  14.6 us (2%)
  starting transfers between devices  14 us (2%)
    pallas_call x4, Pallas kernels, mlp_rest(): pl.pallas_call(functools.partial(mlp_rest_kernel, step), name='mlp_rest',...  276 us
    pallas_call x4, Pallas kernels, attn(): pl.pallas_call(functools.partial(attn_kernel, step, chained), name='attn'...  160 us
    psum x4, waiting for transfers between devices, att(): fns[s] = lax.psum(fn.reshape(2 * SEQ, D), 'tp')  89.1 us
    pallas_call x1, Pallas kernels, mlp_own(): pl.pallas_call(mlp_own_kernel, name='mlp_own', grid_spec=pltpu.PrefetchSc...  66.3 us
    pallas_call x4, Pallas kernels, norm_back(): pl.pallas_call(functools.partial(norm_back_kernel, per), name='norm_back'...  61.8 us
    pallas_call x4, Pallas kernels, out_proj(): pl.pallas_call(out_proj_kernel, name='out_proj', grid=(2 * per,), in_spec...  57.7 us
    pallas_call x2, Pallas kernels, mlp_grad(): pl.pallas_call(functools.partial(grad_kernel, split_rows), name='mlp_grad...  41 us
    ppermute x24, waiting for transfers between devices, swap(): return lax.ppermute(x, 'tp', pairs)  25.2 us
  transfers between devices with their start and end apart: 33, of which 9 were waited for; matrix products, arithmetic and copies ran while one was open for 1% of the time, Pallas kernels for 70%

profile of v1, /device:TPU:0, one launch (start us, length us, event | category | flops | bytes accessed | tf_op | source)
XLA Modules:
  0.0 831.3 jit_solution(10773773468553094618)
XLA Ops:
  7.2 0.8 collective-permute-start
  8.0 3.0 collective-permute-start.4
  11.0 1.5 collective-permute-start.2
  12.5 0.5 collective-permute-start.5
  13.0 1.3 collective-permute-start.3
  14.3 66.3 %mlp_own.1 = (bf16[4096,1280]{1,0:T(8,128)(2,1)}, bf16[4096,1280]{1,0:T(8,128)(2,1)}, bf16[4096,1280]{1,0:T(8,128)(2,1)}, bf16[4096,1280]{1,0:T(8,128)(2,1)}, f3...) custom-call(s32[1]{0:T(128)} %bitcast.1.base, f32[8192,1280]{1,0:T(8,128)} %bitcast.32, f32[8192,1280]{1,0:T(8,128)} %bitcast.42, ...), custom_call_target="tpu_custom_call" | custom-call | flops 53687091200 | bytes 120000000 | tf_op jit(solution)/shard_map/mlp_own/pallas_call | solution.py:91
  80.7 1.6 collective-permute-done.5.refs_6_
  82.4 1.8 collective-permute-start.10
  84.4 0.2 collective-permute-start.6
  84.6 0.3 collective-permute-start.8
  84.9 0.2 collective-permute-start.9
  85.2 20.4 %mlp_grad.2 = (f32[1280,640]{1,0:T(8,128)}, f32[1280,640]{1,0:T(8,128)}) custom-call(bf16[4096,1280]{1,0:T(8,128)(2,1)} %get-tuple-element.64.a.n_in, bf16[4096,1280]{1,0:T(8,128)(2,1)} %get-tuple-element.73.b, f32[4096,1280]{1,0:T(8,128)} %get-tuple-element.68.dep.np_), custom_call_target="tpu_custom_call" | custom-call | flops 13421772800 | bytes 30000000 | tf_op jit(solution)/shard_map/mlp_grad/pallas_call | solution.py:134
  105.6 0.3 collective-permute-start.7
  105.9 15.3 %collective-permute-done.11.refs_10_ = bf16[640,1280]{1,0:T(8,128)(2,1)} collective-permute-done((bf16[640,1280]{1,0:T(8,128)(2,1)}, bf16[640,1280]{1,0:T(8,128)(2,1)}, u32[]{:S(2)}, u32[]{:S(2)}) %collective-permute-start.11) | collective-permute-done | bytes 1638432 | tf_op jit(solution)/shard_map/ppermute | solution.py:524
  121.2 0.5 collective-permute-start.13
  121.7 1.2 copy-done.1
  122.9 2.1 collective-permute-done.12.refs_9_
  125.0 2.3 collective-permute-done.13.refs_11_
  127.4 68.5 %mlp_rest.4 = (f32[1024,1280]{1,0:T(8,128)}, f32[1024,1280]{1,0:T(8,128)}) custom-call(s32[1]{0:T(128)} %bitcast.1.base, bf16[4096,1280]{1,0:T(8,128)(2,1)} %get-tuple-element.64.a.n_in, bf16[4096,1280]{1,0:T(8,128)(2,1)} %get-tuple-element.65.cot_in.b, f32[8192,1280]{1,0:T(8,128)} %bitcast.33, f32[8192,1280]{1,0:T(8,128)} %bitcast.47, ...), custom_call_target="tpu_custom_call" | custom-call | flops 40265318400 | bytes 60000000 | tf_op jit(solution)/shard_map/mlp_rest/pallas_call | solution.py:251
  196.0 0.4 collective-permute-start.14
  196.5 20.6 %mlp_grad.3 = (f32[640,1280]{1,0:T(8,128)}, f32[640,1280]{1,0:T(8,128)}) custom-call(bf16[4096,1280]{1,0:T(8,128)(2,1)} %get-tuple-element.80.a, bf16[4096,1280]{1,0:T(8,128)(2,1)} %get-tuple-element.65.cot_in.b, f32[1024,1280]{1,0:T(8,128)} %get-tuple-element.78.dep.x2o), custom_call_target="tpu_custom_call" | custom-call | flops 13421772800 | bytes 30000000 | tf_op jit(solution)/shard_map/mlp_grad/pallas_call | solution.py:134
  217.1 36.3 %attn.4 = (f32[8192,1280]{1,0:T(8,128)}, f32[8192,1280]{1,0:T(8,128)}, f32[480,1280]{1,0:T(8,128)}, f32[160,1280]{1,0:T(8,128)}, bf16[160,2048]{1,0:T(8,128)(2,1)}, /*index=5*/bf16[2,1024,1280]{2,1,0:T(8,128)(2,1)}) custom-call(s32[1]{0:T(128)} %bitcast.1.base, f32[1024,1280]{1,0:T(8,128)} %get-tuple-element.78.dep.x2o, ...), custom_call_target="tpu_custom_call" | custom-call | flops 24000000000 | bytes 60000000 | tf_op jit(solution)/shard_map/attn/pallas_call | solution.py:396
  253.4 68.6 %mlp_rest.5 = (f32[1024,1280]{1,0:T(8,128)}, f32[1024,1280]{1,0:T(8,128)}) custom-call(s32[1]{0:T(128)} %bitcast.1.base, bf16[4096,1280]{1,0:T(8,128)(2,1)} %get-tuple-element.64.a.n_in, bf16[4096,1280]{1,0:T(8,128)(2,1)} %get-tuple-element.65.cot_in.b, f32[8192,1280]{1,0:T(8,128)} %bitcast.34, f32[8192,1280]{1,0:T(8,128)} %bitcast.48, ...), custom_call_target="tpu_custom_call" | custom-call | flops 40265318400 | bytes 60000000 | tf_op jit(solution)/shard_map/mlp_rest/pallas_call | solution.py:251
  322.3 0.4 collective-permute-start.16
  322.8 14.3 %out_proj.4.refs_0_.refs_1_ = f32[8192,1280]{1,0:T(8,128)} custom-call(f32[8192,1280]{1,0:T(8,128)} %bitcast.35, bf16[1280,2048]{1,0:T(8,128)(2,1)} %all-gather.6.cloned.1.call-done.oT, bf16[1280,1280]{1,0:T(8,128)(2,1)} %all-gather.8.cloned.1.call-done.wo, f32[1024,1280]{1,0:T(8,128)} %get-tuple-element.83.refs_0_.x2o), custom_call_target="tpu_custom_call" | custom-call | flops 6710886400 | bytes 30000000 | tf_op jit(solution)/shard_map/out_proj/pallas_call | solution.py:448
  337.1 3.7 collective-permute-done.16.x2p
  340.7 41.3 %attn.5 = (f32[8192,1280]{1,0:T(8,128)}, f32[8192,1280]{1,0:T(8,128)}, f32[480,1280]{1,0:T(8,128)}, f32[160,1280]{1,0:T(8,128)}, bf16[160,2048]{1,0:T(8,128)(2,1)}, /*index=5*/bf16[2,1024,1280]{2,1,0:T(8,128)(2,1)}) custom-call(s32[1]{0:T(128)} %bitcast.1.base, ...), custom_call_target="tpu_custom_call", output_to_operand_aliasing={{0}: (8, {}), {1}: (9, {}), {2}: (10, {}), {3}: (11, {})} | custom-call | flops 24000000000 | bytes 60000000 | tf_op jit(solution)/shard_map/attn/pallas_call | solution.py:396
  382.1 69.9 %mlp_rest.6 = (f32[1024,1280]{1,0:T(8,128)}, f32[1024,1280]{1,0:T(8,128)}) custom-call(s32[1]{0:T(128)} %bitcast.1.base, bf16[4096,1280]{1,0:T(8,128)(2,1)} %get-tuple-element.64.a.n_in, bf16[4096,1280]{1,0:T(8,128)(2,1)} %get-tuple-element.65.cot_in.b, f32[8192,1280]{1,0:T(8,128)} %bitcast.36, f32[8192,1280]{1,0:T(8,128)} %bitcast.49, ...), custom_call_target="tpu_custom_call" | custom-call | flops 40265318400 | bytes 60000000 | tf_op jit(solution)/shard_map/mlp_rest/pallas_call | solution.py:251
  452.0 0.3 collective-permute-start.19
  452.3 0.3 collective-permute-start.18
  452.7 15.8 %norm_back.4.refs_0_.refs_1_ = f32[8192,1280]{1,0:T(8,128)} custom-call(s32[1]{0:T(128)} %bitcast.1.base, f32[1024,1280]{1,0:T(8,128)} %get-tuple-element.78.dep.x2o, f32[1024,1280]{1,0:T(8,128)} %collective-permute-done.14.x2p, bf16[2048,1280]{1,0:T(8,128)(2,1)} %all-reduce.5.cloned.1.call-done.f, f32[8192,1280]{1,0:T(8,128)} %bitcast.43, ...), custom_call_target="tpu_custom_call" | custom-call | flops 4000000000 | bytes 40000000 | tf_op jit(solution)/shard_map/norm_back/pallas_call | solution.py:498
  468.5 14.2 %out_proj.5.refs_0_.refs_1_ = f32[8192,1280]{1,0:T(8,128)} custom-call(f32[8192,1280]{1,0:T(8,128)} %bitcast.37, bf16[1280,2048]{1,0:T(8,128)(2,1)} %all-gather.10.cloned.1.call-done.oT, bf16[1280,1280]{1,0:T(8,128)(2,1)} %all-gather.8.cloned.1.call-done.wo, f32[8192,1280]{1,0:T(8,128)} %norm_back.4.refs_0_.refs_1_, ...), custom_call_target="tpu_custom_call", output_to_operand_aliasing={{}: (4, {})} | custom-call | flops 6710886400 | bytes 30000000 | tf_op jit(solution)/shard_map/out_proj/pallas_call | solution.py:448
  482.7 41.4 %attn.6 = (f32[8192,1280]{1,0:T(8,128)}, f32[8192,1280]{1,0:T(8,128)}, f32[480,1280]{1,0:T(8,128)}, f32[160,1280]{1,0:T(8,128)}, bf16[160,2048]{1,0:T(8,128)(2,1)}, /*index=5*/bf16[2,1024,1280]{2,1,0:T(8,128)(2,1)}) custom-call(s32[1]{0:T(128)} %bitcast.1.base, ...), custom_call_target="tpu_custom_call", output_to_operand_aliasing={{0}: (8, {}), {1}: (9, {}), {2}: (10, {}), {3}: (11, {})} | custom-call | flops 24000000000 | bytes 60000000 | tf_op jit(solution)/shard_map/attn/pallas_call | solution.py:396
  524.2 68.8 %mlp_rest.7 = (f32[1024,1280]{1,0:T(8,128)}, f32[1024,1280]{1,0:T(8,128)}) custom-call(s32[1]{0:T(128)} %bitcast.1.base, bf16[4096,1280]{1,0:T(8,128)(2,1)} %get-tuple-element.64.a.n_in, bf16[4096,1280]{1,0:T(8,128)(2,1)} %get-tuple-element.65.cot_in.b, f32[8192,1280]{1,0:T(8,128)} %bitcast.38, f32[8192,1280]{1,0:T(8,128)} %bitcast.50, ...), custom_call_target="tpu_custom_call" | custom-call | flops 40265318400 | bytes 60000000 | tf_op jit(solution)/shard_map/mlp_rest/pallas_call | solution.py:251
  593.0 0.5 collective-permute-start.20
  593.6 15.5 %norm_back.5.refs_0_.refs_1_ = f32[8192,1280]{1,0:T(8,128)} custom-call(s32[1]{0:T(128)} %bitcast.1.base, f32[1024,1280]{1,0:T(8,128)} %get-tuple-element.83.refs_0_.x2o, f32[1024,1280]{1,0:T(8,128)} %collective-permute-done.16.x2p, bf16[2048,1280]{1,0:T(8,128)(2,1)} %all-reduce.7.cloned.1.call-done.f, ...), custom_call_target="tpu_custom_call", output_to_operand_aliasing={{}: (6, {})} | custom-call | flops 4000000000 | bytes 40000000 | tf_op jit(solution)/shard_map/norm_back/pallas_call | solution.py:498
  609.1 14.5 %out_proj.6.refs_0_.refs_1_ = f32[8192,1280]{1,0:T(8,128)} custom-call(f32[8192,1280]{1,0:T(8,128)} %bitcast.39, bf16[1280,2048]{1,0:T(8,128)(2,1)} %all-gather.12.cloned.1.call-done.oT, bf16[1280,1280]{1,0:T(8,128)(2,1)} %all-gather.8.cloned.1.call-done.wo, f32[8192,1280]{1,0:T(8,128)} %norm_back.5.refs_0_.refs_1_, ...), custom_call_target="tpu_custom_call", output_to_operand_aliasing={{}: (4, {})} | custom-call | flops 6710886400 | bytes 30000000 | tf_op jit(solution)/shard_map/out_proj/pallas_call | solution.py:448
  623.6 41.5 %attn.7 = (f32[8192,1280]{1,0:T(8,128)}, f32[8192,1280]{1,0:T(8,128)}, f32[480,1280]{1,0:T(8,128)}, f32[160,1280]{1,0:T(8,128)}, bf16[160,2048]{1,0:T(8,128)(2,1)}, /*index=5*/bf16[2,1024,1280]{2,1,0:T(8,128)(2,1)}) custom-call(s32[1]{0:T(128)} %bitcast.1.base, ...), custom_call_target="tpu_custom_call", output_to_operand_aliasing={{0}: (8, {}), {1}: (9, {}), {2}: (10, {}), {3}: (11, {})} | custom-call | flops 24000000000 | bytes 60000000 | tf_op jit(solution)/shard_map/attn/pallas_call | solution.py:396
  665.1 0.3 all-reduce.11.cloned.1.call-start
  665.5 0.5 collective-permute-start.23
  666.0 15.6 %all-reduce.9.cloned.1.call-done.f = bf16[2048,1280]{1,0:T(8,128)(2,1)} async-done(((bf16[2048,1280]{1,0:T(8,128)(2,1)}), bf16[2048,1280]{1,0:T(8,128)(2,1)}) %all-reduce.9.cloned.1.call-update) | async-done | bytes 5242896 | tf_op jit(solution)/shard_map/psum | solution.py:564
  681.7 4.1 add_bitcast_fusion.1
  685.8 4.1 add_bitcast_fusion
  689.8 15.3 %norm_back.6.refs_0_.refs_1_ = f32[8192,1280]{1,0:T(8,128)} custom-call(s32[1]{0:T(128)} %bitcast.1.base, f32[1024,1280]{1,0:T(8,128)} %get-tuple-element.90.refs_0_.x2o, f32[1024,1280]{1,0:T(8,128)} %collective-permute-done.18.x2p, bf16[2048,1280]{1,0:T(8,128)(2,1)} %all-reduce.9.cloned.1.call-done.f, ...), custom_call_target="tpu_custom_call", output_to_operand_aliasing={{}: (6, {})} | custom-call | flops 4000000000 | bytes 40000000 | tf_op jit(solution)/shard_map/norm_back/pallas_call | solution.py:498
  705.1 15.8 %all-gather.14.cloned.1.call-done.oT = bf16[1280,2048]{1,0:T(8,128)(2,1)} async-done(((bf16[160,2048]{1,0:T(8,128)(2,1)}), bf16[1280,2048]{1,0:T(8,128)(2,1)}) %all-gather.14.cloned.1.call-update) | async-done | bytes 5242896 | tf_op jit(solution)/shard_map/all_gather | solution.py:561
  720.9 14.8 %out_proj.7.refs_0_ = f32[8192,1280]{1,0:T(8,128)} custom-call(f32[8192,1280]{1,0:T(8,128)} %bitcast.40, bf16[1280,2048]{1,0:T(8,128)(2,1)} %all-gather.14.cloned.1.call-done.oT, bf16[1280,1280]{1,0:T(8,128)(2,1)} %all-gather.8.cloned.1.call-done.wo, f32[8192,1280]{1,0:T(8,128)} %norm_back.6.refs_0_.refs_1_, ...), custom_call_target="tpu_custom_call", output_to_operand_aliasing={{}: (4, {})} | custom-call | flops 6710886400 | bytes 30000000 | tf_op jit(solution)/shard_map/out_proj/pallas_call | solution.py:448
  735.7 73.4 %all-reduce.11.cloned.1.call-done.f = bf16[2048,1280]{1,0:T(8,128)(2,1)} async-done(((bf16[2048,1280]{1,0:T(8,128)(2,1)}), bf16[2048,1280]{1,0:T(8,128)(2,1)}) %all-reduce.11.cloned.1.call-update) | async-done | bytes 5242896 | tf_op jit(solution)/shard_map/psum | solution.py:564
  809.1 15.2 %norm_back.7 = f32[8192,1280]{1,0:T(8,128)} custom-call(s32[1]{0:T(128)} %bitcast.1.base, f32[1024,1280]{1,0:T(8,128)} %get-tuple-element.100.refs_0_.x2o, f32[1024,1280]{1,0:T(8,128)} %collective-permute-done.20.x2p, bf16[2048,1280]{1,0:T(8,128)(2,1)} %all-reduce.11.cloned.1.call-done.f, f32[8192,1280]{1,0:T(8,128)} %bitcast.46, ...), custom_call_target="tpu_custom_call", output_to_operand_aliasing={{}: (6, {})} | custom-call | flops 4000000000 | bytes 40000000 | tf_op jit(solution)/shard_map/norm_back/pallas_call | solution.py:498
  (56 shorter events, 1.4 us)
Async XLA Ops:
  7.2 315.6 %all-gather.8.cloned.1.call-start = ((), (), s32[]{:S(2)}) async-start(), calls=%async_computation.1 | async-start | bytes 3686400 | tf_op jit(solution)/shard_map/all_gather | solution.py:547
  7.2 5.8 collective-permute-start
  8.0 6.3 collective-permute-start.1
  8.0 72.6 %collective-permute-start.4 = (bf16[1280,640]{1,0:T(8,128)(2,1)}, bf16[1280,640]{1,0:T(8,128)(2,1)S(1)}, u32[]{:S(2)}, u32[]{:S(2)}) collective-permute-start(bf16[1280,640]{1,0:T(8,128)(2,1)} %bitcast.73), channel_id=1, source_target_pairs={{0,4},{1,3},{2,6},{3,1},{4,0},{5,7},{6,2},{7,5},{8,12},{9,11},{10,... | collective-permute-start | bytes 4915208 | tf_op jit(solution)/shard_map/ppermute | solution.py:524
  11.0 69.7 %collective-permute-start.2 = (bf16[1280,640]{1,0:T(8,128)(2,1)}, bf16[1280,640]{1,0:T(8,128)(2,1)}, u32[]{:S(2)}, u32[]{:S(2)}) collective-permute-start(bf16[1280,640]{1,0:T(8,128)(2,1)} %bitcast.74), channel_id=1, source_target_pairs={{0,2},{1,5},{2,0},{3,7},{4,6},{5,1},{6,4},{7,3},{8,10},{9,13},{10,... | collective-permute-start | bytes 4915208 | tf_op jit(solution)/shard_map/ppermute | solution.py:524
  12.5 69.8 %collective-permute-start.5 = (bf16[640,1280]{1,0:T(8,128)(2,1)}, bf16[640,1280]{1,0:T(8,128)(2,1)}, u32[]{:S(2)}, u32[]{:S(2)}) collective-permute-start(bf16[640,1280]{1,0:T(8,128)(2,1)} %bitcast.77), channel_id=1, source_target_pairs={{0,4},{1,3},{2,6},{3,1},{4,0},{5,7},{6,2},{7,5},{8,12},{9,11},{10,... | collective-permute-start | bytes 4915208 | tf_op jit(solution)/shard_map/ppermute | solution.py:524
  13.0 69.4 %collective-permute-start.3 = (bf16[640,1280]{1,0:T(8,128)(2,1)}, bf16[640,1280]{1,0:T(8,128)(2,1)}, u32[]{:S(2)}, u32[]{:S(2)}) collective-permute-start(bf16[640,1280]{1,0:T(8,128)(2,1)} %bitcast.78), channel_id=1, source_target_pairs={{0,2},{1,5},{2,0},{3,7},{4,6},{5,1},{6,4},{7,3},{8,10},{9,13},{10,... | collective-permute-start | bytes 4915208 | tf_op jit(solution)/shard_map/ppermute | solution.py:524
  80.6 24.9 %copy-start = (bf16[1280,640]{1,0:T(8,128)(2,1)}, bf16[1280,640]{1,0:T(8,128)(2,1)S(1)}, u32[]{:S(2)}) copy-start(bf16[1280,640]{1,0:T(8,128)(2,1)S(1)} %collective-permute-done.4.refs_4_) | copy-start | bytes 4915204
  82.4 23.2 %collective-permute-start.10 = (bf16[1280,640]{1,0:T(8,128)(2,1)S(1)}, bf16[1280,640]{1,0:T(8,128)(2,1)}, u32[]{:S(2)}, u32[]{:S(2)}) collective-permute-start(bf16[1280,640]{1,0:T(8,128)(2,1)S(1)} %collective-permute-done.4.refs_4_), channel_id=1, source_target_pairs={{0,2},{1,5},{2,0},{3,7},{4,6},{5,1},{6,4},{7,3},{8,10},{9,13},{10,... | collective-permute-start | bytes 4915208 | tf_op jit(solution)/shard_map/ppermute | solution.py:524
  84.2 37.0 %collective-permute-start.11 = (bf16[640,1280]{1,0:T(8,128)(2,1)}, bf16[640,1280]{1,0:T(8,128)(2,1)}, u32[]{:S(2)}, u32[]{:S(2)}) collective-permute-start(bf16[640,1280]{1,0:T(8,128)(2,1)} %collective-permute-done.5.refs_6_), channel_id=1, source_target_pairs={{0,2},{1,5},{2,0},{3,7},{4,6},{5,1},{6,4},{7,3},{8,10},{9,13},{10,... | collective-permute-start | bytes 4915208 | tf_op jit(solution)/shard_map/ppermute | solution.py:524
  84.4 36.8 %collective-permute-start.6 = (bf16[1280,640]{1,0:T(8,128)(2,1)}, bf16[1280,640]{1,0:T(8,128)(2,1)}, u32[]{:S(2)}, u32[]{:S(2)}) collective-permute-start(bf16[1280,640]{1,0:T(8,128)(2,1)} %collective-permute-done.2.refs_0_), channel_id=1, source_target_pairs={{0,1},{1,0},{2,3},{3,2},{4,5},{5,4},{6,7},{7,6},{8,9},{9,8},{10,11... | collective-permute-start | bytes 4915208 | tf_op jit(solution)/shard_map/ppermute | solution.py:524
  84.6 37.0 %collective-permute-start.8 = (bf16[1280,640]{1,0:T(8,128)(2,1)S(1)}, bf16[1280,640]{1,0:T(8,128)(2,1)}, u32[]{:S(2)}, u32[]{:S(2)}) collective-permute-start(bf16[1280,640]{1,0:T(8,128)(2,1)S(1)} %collective-permute-done.4.refs_4_), channel_id=1, source_target_pairs={{0,1},{1,0},{2,3},{3,2},{4,5},{5,4},{6,7},{7,6},{8,9},{9,8},{10,11... | collective-permute-start | bytes 4915208 | tf_op jit(solution)/shard_map/ppermute | solution.py:524
  84.9 38.0 %collective-permute-start.9 = (bf16[640,1280]{1,0:T(8,128)(2,1)}, bf16[640,1280]{1,0:T(8,128)(2,1)}, u32[]{:S(2)}, u32[]{:S(2)}) collective-permute-start(bf16[640,1280]{1,0:T(8,128)(2,1)} %collective-permute-done.5.refs_6_), channel_id=1, source_target_pairs={{0,1},{1,0},{2,3},{3,2},{4,5},{5,4},{6,7},{7,6},{8,9},{9,8},{10,11... | collective-permute-start | bytes 4915208 | tf_op jit(solution)/shard_map/ppermute | solution.py:524
  105.6 16.1 %collective-permute-start.7 = (bf16[640,1280]{1,0:T(8,128)(2,1)}, bf16[640,1280]{1,0:T(8,128)(2,1)S(1)}, u32[]{:S(2)}, u32[]{:S(2)}) collective-permute-start(bf16[640,1280]{1,0:T(8,128)(2,1)} %collective-permute-done.3.refs_2_), channel_id=1, source_target_pairs={{0,1},{1,0},{2,3},{3,2},{4,5},{5,4},{6,7},{7,6},{8,9},{9,8},{10,11... | collective-permute-start | bytes 4915208 | tf_op jit(solution)/shard_map/ppermute | solution.py:524
  121.2 3.8 collective-permute-start.12
  121.2 6.2 collective-permute-start.13
  121.7 1.2 copy-start.1
  195.9 21.2 %collective-permute-start.15 = (f32[1024,1280]{1,0:T(8,128)}, f32[1024,1280]{1,0:T(8,128)}, u32[]{:S(2)}, u32[]{:S(2)}) collective-permute-start(f32[1024,1280]{1,0:T(8,128)} %get-tuple-element.79.d1o), channel_id=1, source_target_pairs={{0,1},{1,0},{2,3},{3,2},{4,5},{5,4},{6,7},{7,6},{8,9},{9,8},{10,11... | collective-permute-start | bytes 15728648 | tf_op jit(solution)/shard_map/ppermute | solution.py:524
  196.0 21.1 %collective-permute-start.14 = (f32[1024,1280]{1,0:T(8,128)}, f32[1024,1280]{1,0:T(8,128)}, u32[]{:S(2)}, u32[]{:S(2)}) collective-permute-start(f32[1024,1280]{1,0:T(8,128)} %get-tuple-element.78.dep.x2o), channel_id=1, source_target_pairs={{0,1},{1,0},{2,3},{3,2},{4,5},{5,4},{6,7},{7,6},{8,9},{9,8},{10,11... | collective-permute-start | bytes 15728648 | tf_op jit(solution)/shard_map/ppermute | solution.py:524
  196.4 126.3 %all-gather.6.cloned.1.call-start = ((), (), s32[]{:S(2)}) async-start(), calls=%async_computation | async-start | bytes 5898240 | tf_op jit(solution)/shard_map/all_gather | solution.py:561
  253.4 199.2 %all-reduce.5.cloned.1.call-start = ((), (), s32[]{:S(2)}) async-start(), calls=%async_computation.3 | async-start | bytes 10485760 | tf_op jit(solution)/shard_map/psum | solution.py:564
  322.1 15.0 %collective-permute-start.17 = (f32[1024,1280]{1,0:T(8,128)}, f32[1024,1280]{1,0:T(8,128)}, u32[]{:S(2)}, u32[]{:S(2)}) collective-permute-start(f32[1024,1280]{1,0:T(8,128)} %get-tuple-element.84.d1o), channel_id=1, source_target_pairs={{0,1},{1,0},{2,3},{3,2},{4,5},{5,4},{6,7},{7,6},{8,9},{9,8},{10,11... | collective-permute-start | bytes 15728648 | tf_op jit(solution)/shard_map/ppermute | solution.py:524
  322.3 18.5 %collective-permute-start.16 = (f32[1024,1280]{1,0:T(8,128)}, f32[1024,1280]{1,0:T(8,128)}, u32[]{:S(2)}, u32[]{:S(2)}) collective-permute-start(f32[1024,1280]{1,0:T(8,128)} %get-tuple-element.83.refs_0_.x2o), channel_id=1, source_target_pairs={{0,1},{1,0},{2,3},{3,2},{4,5},{5,4},{6,7},{7,6},{8,9},{9,8},{10,11... | collective-permute-start | bytes 15728648 | tf_op jit(solution)/shard_map/ppermute | solution.py:524
  322.7 145.8 %all-gather.10.cloned.1.call-start = ((), (), s32[]{:S(2)}) async-start(), calls=%async_computation.2 | async-start | bytes 5898240 | tf_op jit(solution)/shard_map/all_gather | solution.py:561
  382.1 211.5 %all-reduce.7.cloned.1.call-start = ((), (), s32[]{:S(2)}) async-start(), calls=%async_computation.5 | async-start | bytes 10485760 | tf_op jit(solution)/shard_map/psum | solution.py:564
  452.0 30.6 %collective-permute-start.19 = (f32[1024,1280]{1,0:T(8,128)}, f32[1024,1280]{1,0:T(8,128)}, u32[]{:S(2)}, u32[]{:S(2)}) collective-permute-start(f32[1024,1280]{1,0:T(8,128)} %get-tuple-element.91.d1o), channel_id=1, source_target_pairs={{0,1},{1,0},{2,3},{3,2},{4,5},{5,4},{6,7},{7,6},{8,9},{9,8},{10,11... | collective-permute-start | bytes 15728648 | tf_op jit(solution)/shard_map/ppermute | solution.py:524
  452.3 30.3 %collective-permute-start.18 = (f32[1024,1280]{1,0:T(8,128)}, f32[1024,1280]{1,0:T(8,128)}, u32[]{:S(2)}, u32[]{:S(2)}) collective-permute-start(f32[1024,1280]{1,0:T(8,128)} %get-tuple-element.90.refs_0_.x2o), channel_id=1, source_target_pairs={{0,1},{1,0},{2,3},{3,2},{4,5},{5,4},{6,7},{7,6},{8,9},{9,8},{10,11... | collective-permute-start | bytes 15728648 | tf_op jit(solution)/shard_map/ppermute | solution.py:524
  452.6 156.5 %all-gather.12.cloned.1.call-start = ((), (), s32[]{:S(2)}) async-start(), calls=%async_computation.4 | async-start | bytes 5898240 | tf_op jit(solution)/shard_map/all_gather | solution.py:561
  524.1 157.5 %all-reduce.9.cloned.1.call-start = ((), (), s32[]{:S(2)}) async-start(), calls=%async_computation.7 | async-start | bytes 10485760 | tf_op jit(solution)/shard_map/psum | solution.py:564
  593.0 30.6 %collective-permute-start.21 = (f32[1024,1280]{1,0:T(8,128)}, f32[1024,1280]{1,0:T(8,128)}, u32[]{:S(2)}, u32[]{:S(2)}) collective-permute-start(f32[1024,1280]{1,0:T(8,128)} %get-tuple-element.101.d1o), channel_id=1, source_target_pairs={{0,1},{1,0},{2,3},{3,2},{4,5},{5,4},{6,7},{7,6},{8,9},{9,8},{10,11... | collective-permute-start | bytes 15728648 | tf_op jit(solution)/shard_map/ppermute | solution.py:524
  593.0 30.5 %collective-permute-start.20 = (f32[1024,1280]{1,0:T(8,128)}, f32[1024,1280]{1,0:T(8,128)}, u32[]{:S(2)}, u32[]{:S(2)}) collective-permute-start(f32[1024,1280]{1,0:T(8,128)} %get-tuple-element.100.refs_0_.x2o), channel_id=1, source_target_pairs={{0,1},{1,0},{2,3},{3,2},{4,5},{5,4},{6,7},{7,6},{8,9},{9,8},{10,11... | collective-permute-start | bytes 15728648 | tf_op jit(solution)/shard_map/ppermute | solution.py:524
  593.6 127.3 %all-gather.14.cloned.1.call-start = ((), (), s32[]{:S(2)}) async-start(), calls=%async_computation.6 | async-start | bytes 5898240 | tf_op jit(solution)/shard_map/all_gather | solution.py:561
  665.1 16.6 %copy-start.2 = (f32[1280,640]{1,0:T(8,128)S(1)}, f32[1280,640]{1,0:T(8,128)}, u32[]{:S(2)}) copy-start(f32[1280,640]{1,0:T(8,128)} %get-tuple-element.77.refs_12_) | copy-start | bytes 9830404
  665.1 144.0 %all-reduce.11.cloned.1.call-start = ((), (), s32[]{:S(2)}) async-start(), calls=%async_computation.8 | async-start | bytes 10485760 | tf_op jit(solution)/shard_map/psum | solution.py:564
  665.4 16.2 %collective-permute-start.22 = (f32[1280,640]{1,0:T(8,128)}, f32[1280,640]{1,0:T(8,128)}, u32[]{:S(2)}, u32[]{:S(2)}) collective-permute-start(f32[1280,640]{1,0:T(8,128)} %get-tuple-element.118), channel_id=1, source_target_pairs={{0,1},{1,0},{2,3},{3,2},{4,5},{5,4},{6,7},{7,6},{8,9},{9,8},{10,11... | collective-permute-start | bytes 9830408 | tf_op jit(solution)/shard_map/ppermute | solution.py:524
  665.5 20.3 %collective-permute-start.23 = (f32[640,1280]{1,0:T(8,128)}, f32[640,1280]{1,0:T(8,128)}, u32[]{:S(2)}, u32[]{:S(2)}) collective-permute-start(f32[640,1280]{1,0:T(8,128)} %get-tuple-element.119), channel_id=1, source_target_pairs={{0,1},{1,0},{2,3},{3,2},{4,5},{5,4},{6,7},{7,6},{8,9},{9,8},{10,11... | collective-permute-start | bytes 9830408 | tf_op jit(solution)/shard_map/ppermute | solution.py:524
  681.6 4.1 copy-start.3
Sparse Core Ops, SparseCore 0:
  196.6 30.5 all-gather.7
  253.5 38.7 all-gather.5
  322.8 86.3 all-reduce.4
  410.9 37.4 all-gather.9
  452.7 86.7 all-reduce.6
  541.2 37.4 all-gather.11
  593.7 87.8 all-reduce.8
  683.4 37.3 all-gather.13
  724.2 84.9 all-reduce.10

commit v2 on v1

v2 whole, which is shorter than its diff:
```python
import functools
import math

import jax
import jax.numpy as jnp
from jax import lax
from jax.experimental import pallas as pl
from jax.experimental.pallas import tpu as pltpu
from jax.sharding import PartitionSpec as P

F32, BF16 = jnp.float32, jnp.bfloat16
NORM_EPS = 1e-6
GELU_C = math.sqrt(2.0 / math.pi)
GELU_K = 0.044715
D = 1280
SEQ = 1024
HEAD = 80
HEADS_DEV = 2
QKV = 3 * HEAD * HEADS_DEV
OUT = HEAD * HEADS_DEV
FFD = 640
ROWS = 512
STEPS = 4
SCALE = 1.0 / math.sqrt(HEAD)
VMEM_CAP = 62 * 1024 * 1024


def dot(a, b, dims=((1,), (0,))):
    return lax.dot_general(a, b, (dims, ((), ())), preferred_element_type=F32)


NT = ((1,), (1,))
TN = ((0,), (0,))


def inv_rms(x):
    return lax.rsqrt(jnp.mean(x * x, axis=-1, keepdims=True) + NORM_EPS)


def gelu_pair(h):
    sq = h * h
    t = jnp.tanh(h * (GELU_C + (GELU_C * GELU_K) * sq))
    cdf = 0.5 + 0.5 * t
    act = h * cdf
    slope = cdf + (0.5 * h) * (1.0 - t * t) * (GELU_C + (3.0 * GELU_C * GELU_K) * sq)
    return act.astype(BF16), slope


def cost(flops, nbytes):
    return pl.CostEstimate(flops=int(flops), bytes_accessed=int(nbytes), transcendentals=0)


def any_spec():
    return pl.BlockSpec(memory_space=pl.ANY)


def params(**kw):
    return pltpu.CompilerParams(vmem_limit_bytes=VMEM_CAP, **kw)


def mlp_own_kernel(base, y1, c2, w1o, w1p, w2o, w2p, n_out, cot_out, act_out, dh_out, gp_out, np_out, w1, w2, sems):
    @pl.when(pl.program_id(0) == 0)
    def _():
        cps = [
            pltpu.make_async_copy(w1o, w1.at[:, pl.ds(0, FFD)], sems.at[0]),
            pltpu.make_async_copy(w1p, w1.at[:, pl.ds(FFD, FFD)], sems.at[1]),
            pltpu.make_async_copy(w2o, w2.at[pl.ds(0, FFD), :], sems.at[2]),
            pltpu.make_async_copy(w2p, w2.at[pl.ds(FFD, FFD), :], sems.at[3]),
        ]
        for cp in cps:
            cp.start()
        for cp in cps:
            cp.wait()

    cot = c2[...].astype(BF16)
    cot_out[...] = cot
    da = dot(cot, w2[...], NT)
    y = y1[...]
    n = (y * inv_rms(y)).astype(BF16)
    n_out[...] = n
    act, slope = gelu_pair(dot(n, w1[...]))
    act_out[...] = act
    dh = (da * slope).astype(BF16)
    dh_out[...] = dh
    gp_out[...] = dot(act, w2[...])
    np_out[...] = dot(dh, w1[...], NT)


def mlp_own(core, y1, c2, w1o, w1p, w2o, w2p):
    half = STEPS * SEQ
    blocks = half // ROWS
    row_in = pl.BlockSpec((ROWS, D), lambda i, base: (base[0] * blocks + i, 0))
    row_out = pl.BlockSpec((ROWS, D), lambda i, base: (i, 0))
    return pl.pallas_call(
        mlp_own_kernel,
        name="mlp_own",
        grid_spec=pltpu.PrefetchScalarGridSpec(
            num_scalar_prefetch=1,
            grid=(blocks,),
            in_specs=[row_in, row_in] + [any_spec()] * 4,
            out_specs=[row_out] * 6,
            scratch_shapes=[
                pltpu.VMEM((D, 2 * FFD), BF16),
                pltpu.VMEM((2 * FFD, D), BF16),
                pltpu.SemaphoreType.DMA((4,)),
            ],
        ),
        out_shape=[jax.ShapeDtypeStruct((half, D), BF16)] * 4 + [jax.ShapeDtypeStruct((half, D), F32)] * 2,
        compiler_params=params(dimension_semantics=("arbitrary",)),
        cost_estimate=cost(4 * 2 * half * D * 2 * FFD, 120e6),
    )(core, y1, c2, w1o, w1p, w2o, w2p)


def grad_kernel(split_rows, a, b, dep, own, peer, acc, sems):
    i = pl.program_id(0)

    @pl.when(i == 0)
    def _():
        acc[...] = jnp.zeros_like(acc)

    acc[...] += dot(a[...], b[...], TN)

    @pl.when(i == pl.num_programs(0) - 1)
    def _():
        part = lambda k: acc.at[pl.ds(k * FFD, FFD), :] if split_rows else acc.at[:, pl.ds(k * FFD, FFD)]
        cps = [pltpu.make_async_copy(part(0), own, sems.at[0]), pltpu.make_async_copy(part(1), peer, sems.at[1])]
        for cp in cps:
            cp.start()
        for cp in cps:
            cp.wait()


def mlp_grad(split_rows, a, b, dep):
    half = STEPS * SEQ
    row = pl.BlockSpec((SEQ, D), lambda i: (i, 0))
    shape = (FFD, D) if split_rows else (D, FFD)
    return pl.pallas_call(
        functools.partial(grad_kernel, split_rows),
        name="mlp_grad",
        grid=(half // SEQ,),
        in_specs=[row, row, any_spec()],
        out_specs=[any_spec()] * 2,
        scratch_shapes=[pltpu.VMEM((D, 2 * FFD), F32), pltpu.SemaphoreType.DMA((2,))],
        out_shape=[jax.ShapeDtypeStruct(shape, F32)] * 2,
        compiler_params=params(dimension_semantics=("arbitrary",)),
        cost_estimate=cost(2 * half * D * 2 * FFD, 30e6),
    )(a, b, dep)


def mlp_rest_kernel(step, chunks, resumed, final, base, n_in, cot_in, y1, y2, c1, gp, np_, *refs):
    ws = refs[: 4 * chunks]
    refs = refs[4 * chunks :]
    part = refs[:2]
    refs = refs[2:] if resumed else refs
    out_g, out_n = refs[1:3]
    w1, w2, late, accg, accn, wsem, lsem, osem = refs[3:]
    i = pl.program_id(0)
    row = pl.multiple_of(base[0] * (STEPS * SEQ) + step * SEQ + i * ROWS, ROWS)
    loc = pl.multiple_of(step * SEQ + i * ROWS, ROWS)
    out_row = pl.multiple_of(i * ROWS, ROWS)

    def w_copies(k):
        a1o, a1p, a2o, a2p = ws[4 * k : 4 * k + 4]
        return [
            pltpu.make_async_copy(a1o, w1.at[k, :, pl.ds(0, FFD)], wsem.at[k, 0]),
            pltpu.make_async_copy(a1p, w1.at[k, :, pl.ds(FFD, FFD)], wsem.at[k, 1]),
            pltpu.make_async_copy(a2o, w2.at[k, pl.ds(0, FFD), :], wsem.at[k, 2]),
            pltpu.make_async_copy(a2p, w2.at[k, pl.ds(FFD, FFD), :], wsem.at[k, 3]),
        ]

    def start(cps):
        for cp in cps:
            cp.start()

    def wait(cps):
        for cp in cps:
            cp.wait()

    srcs = [(np_, loc), (y1, row), (c1, row), (gp, loc), (y2, row)] if final else []
    if resumed:
        srcs += [(part[0], out_row), (part[1], out_row)]
    late_copies = [
        pltpu.make_async_copy(src.at[pl.ds(at, ROWS), :], late.at[j], lsem.at[j]) for j, (src, at) in enumerate(srcs)
    ]
    outs = [
        pltpu.make_async_copy(accg, out_g.at[pl.ds(out_row, ROWS), :], osem.at[0]),
        pltpu.make_async_copy(accn, out_n.at[pl.ds(out_row, ROWS), :], osem.at[1]),
    ]

    def arrive(k):
        @pl.when(i == 0)
        def _():
            if k == 0:
                start(w_copies(0))
            wait(w_copies(k))
            if k + 1 < chunks:
                start(w_copies(k + 1))

    for k in range(chunks):
        arrive(k)
        if k == chunks - 1:
            start(late_copies)
        if k == min(1, chunks - 1):
            @pl.when(i > 0)
            def _():
                wait(outs)
        last = final and k == chunks - 1
        act, slope = gelu_pair(dot(n_in[...], w1[k]))
        dh = (dot(cot_in[...], w2[k], NT) * slope).astype(BF16)
        if last:
            wait(late_copies)
        gn = dot(dh, w1[k], NT)
        if not last:
            accn[...] = gn if k == 0 else accn[...] + gn
            g = dot(act, w2[k])
            accg[...] = g if k == 0 else accg[...] + g
            continue
        prev_n = late[6] if resumed else accn[...]
        gn = prev_n + (late[0] + gn)
        y = late[1]
        r = inv_rms(y)
        nf = y * r
        accn[...] = late[2] + r * (gn - nf * jnp.mean(nf * gn, axis=-1, keepdims=True))
        prev_g = late[5] if resumed else accg[...]
        accg[...] = late[4] - (prev_g + (late[3] + dot(act, w2[k])))
    start(outs)

    @pl.when(i == pl.num_programs(0) - 1)
    def _():
        wait(outs)


def mlp_rest(step, core, n_in, cot_in, y1, y2, c1, gp, np_, ws, part, dep, final):
    blocks = SEQ // ROWS
    chunks = len(ws) // 4
    resumed = part is not None
    lates = (5 if final else 0) + (2 if resumed else 0)
    row_in = pl.BlockSpec((ROWS, D), lambda i, base: (step * blocks + i, 0))
    ins = [y1, y2, c1, gp, np_, *ws, *(part or ()), dep]
    return pl.pallas_call(
        functools.partial(mlp_rest_kernel, step, chunks, resumed, final),
        name="mlp_rest",
        grid_spec=pltpu.PrefetchScalarGridSpec(
            num_scalar_prefetch=1,
            grid=(blocks,),
            in_specs=[row_in, row_in] + [any_spec()] * len(ins),
            out_specs=[any_spec()] * 2,
            scratch_shapes=[
                pltpu.VMEM((chunks, D, 2 * FFD), BF16),
                pltpu.VMEM((chunks, 2 * FFD, D), BF16),
                pltpu.VMEM((max(lates, 1), ROWS, D), F32),
                pltpu.VMEM((ROWS, D), F32),
                pltpu.VMEM((ROWS, D), F32),
                pltpu.SemaphoreType.DMA((chunks, 4)),
                pltpu.SemaphoreType.DMA((max(lates, 1),)),
                pltpu.SemaphoreType.DMA((2,)),
            ],
        ),
        out_shape=[jax.ShapeDtypeStruct((SEQ, D), F32)] * 2,
        compiler_params=params(dimension_semantics=("arbitrary",)),
        cost_estimate=cost(chunks * 4 * 2 * SEQ * D * 2 * FFD, 60e6),
    )(core, n_in, cot_in, *ins)


PARTS = 2


def attn_kernel(step, peer, chained, base, x2, d1, wq, wo, *refs):
    nin = (0 if peer else 2) + (4 if chained else 0) + 1
    fr = None if peer else refs[0]
    refs = refs[nin:]
    nout = 6 if peer else 7
    x2_out, d1_out, aq, ao, oT_out = refs[:5]
    fouts = refs[5:nout]
    scr = refs[nout:]
    xb, cb, n2, cot, qkvT, dqkvT, dOT, oT, kb, vb, dk, dv, fnb, accq, acco, isem, wsem, osem, asem = scr[:19]
    frb, frsem = (None, None) if peer else scr[19:]
    owner = 1 - base[0] if peer else base[0]
    row = pl.multiple_of(owner * (STEPS * SEQ) + step * SEQ, SEQ)
    size = SEQ // PARTS

    def start(cps):
        for cp in cps:
            cp.start()

    def wait(cps):
        for cp in cps:
            cp.wait()

    def in_copy(src, dst, which, r):
        at = pl.ds(r * size, size)
        return pltpu.make_async_copy(src.at[at, :], dst.at[at, :], isem.at[which, r])

    xin = [in_copy(x2, xb, 0, r) for r in range(PARTS)]
    cin = [in_copy(d1, cb, 1, r) for r in range(PARTS)]
    echo = [
        pltpu.make_async_copy(xb, x2_out.at[pl.ds(row, SEQ), :], wsem.at[0]),
        pltpu.make_async_copy(cb, d1_out.at[pl.ds(row, SEQ), :], wsem.at[1]),
    ]
    acc_out = [pltpu.make_async_copy(accq, aq, asem.at[0]), pltpu.make_async_copy(acco, ao, asem.at[1])]
    col = pl.multiple_of(owner * SEQ, SEQ)
    o_out = pltpu.make_async_copy(oT, oT_out.at[:, pl.ds(col, SEQ)], osem.at[0])
    queue = xin + cin
    start(queue[:2])
    if chained:
        acc_in = [pltpu.make_async_copy(aq, accq, asem.at[0]), pltpu.make_async_copy(ao, acco, asem.at[1])]
    for r in range(PARTS):
        xin[r].wait()
        start(queue[r + 2 : r + 3])
        rows = pl.ds(r * size, size)
        x = xb[rows, :]
        n = (x * inv_rms(x)).astype(BF16)
        n2[rows, :] = n
        qkvT[:, rows] = dot(wq[...], n, NT).astype(BF16)
    for r in range(PARTS):
        cin[r].wait()
        start(queue[r + PARTS + 2 : r + PARTS + 3])
        rows = pl.ds(r * size, size)
        c = cb[rows, :].astype(BF16)
        cot[rows, :] = c
        dOT[:, rows] = dot(c, wo[...], NT).astype(BF16).T
    start(echo)
    if chained:
        start(acc_in)
    if not peer:
        fr_in = pltpu.make_async_copy(fr, frb, frsem.at[0])
        fr_in.start()

    def head(h, _):
        at = pl.multiple_of(h * (3 * HEAD), 16)
        oat = pl.multiple_of(h * HEAD, 16)
        kb[...] = qkvT[pl.ds(at + HEAD, HEAD), :].T
        vb[...] = qkvT[pl.ds(at + 2 * HEAD, HEAD), :].T
        for qb in range(SEQ // ROWS):
            cols = pl.ds(qb * ROWS, ROWS)
            qT = qkvT[pl.ds(at, HEAD), cols]
            gT = dOT[pl.ds(oat, HEAD), cols]
            s = dot(kb[...], qT)
            m = jnp.max(s, axis=0, keepdims=True)
            p = jnp.exp2((s - m) * (SCALE * math.log2(math.e)))
            p = p * (1.0 / jnp.sum(p, axis=0, keepdims=True))
            pb = p.astype(BF16)
            dp = dot(vb[...], gT)
            r = jnp.sum(dp * p, axis=0, keepdims=True)
            ds = (p * (dp - r) * SCALE).astype(BF16)
            oT[pl.ds(oat, HEAD), cols] = dot(qkvT[pl.ds(at + 2 * HEAD, HEAD), :], pb).astype(BF16)
            dvp = dot(pb, gT.T)
            dqkvT[pl.ds(at, HEAD), cols] = dot(qkvT[pl.ds(at + HEAD, HEAD), :], ds).astype(BF16)
            dkp = dot(ds, qT.T)
            if qb == 0:
                dv[...] = dvp
                dk[...] = dkp
            else:
                dqkvT[pl.ds(at + 2 * HEAD, HEAD), :] = (dv[...] + dvp).astype(BF16).T
                dqkvT[pl.ds(at + HEAD, HEAD), :] = (dk[...] + dkp).astype(BF16).T
        return 0

    lax.fori_loop(0, HEADS_DEV, head, 0)
    o_out.start()
    if peer:
        fnb[...] = dot(dqkvT[...], wq[...], TN).astype(BF16)
        f_out = [pltpu.make_async_copy(fnb, fouts[0], osem.at[1])]
    else:
        fr_in.wait()
        fnb[...] = dot(dqkvT[...], wq[...], TN) + frb[...].astype(F32)
        half = SEQ // 2
        go = pl.multiple_of((1 - base[1]) * half, half)
        stay = pl.multiple_of(base[1] * half, half)
        frb[pl.ds(0, half), :] = fnb[pl.ds(go, half), :].astype(BF16)
        f_out = [
            pltpu.make_async_copy(frb.at[pl.ds(0, half), :], fouts[0], osem.at[1]),
            pltpu.make_async_copy(fnb.at[pl.ds(stay, half), :], fouts[1], osem.at[2]),
        ]
    start(f_out)
    dq = dot(dqkvT[...], n2[...])
    do = dot(oT[...], cot[...])
    if chained:
        wait(acc_in)
        accq[...] += dq
        acco[...] += do
    else:
        accq[...] = dq
        acco[...] = do
    start(acc_out)
    wait(acc_out + f_out + [o_out] + echo)


def attn(step, peer, core, x2, d1, wq, wo, fr, oT, dep, chain):
    full = jax.ShapeDtypeStruct((2 * STEPS * SEQ, D), F32)
    whole = lambda shape: pl.BlockSpec(shape, lambda i, base: (0, 0))
    chained = chain is not None
    ins = [core, x2, d1, wq, wo] + ([] if peer else [fr, oT])
    first = len(ins)
    ins += (list(chain) if chained else []) + [dep]
    alias = {first + k: k for k in range(4)} if chained else {}
    if not peer:
        alias[6] = 4
    half = SEQ // 2
    if peer:
        fshapes = [jax.ShapeDtypeStruct((SEQ, D), BF16)]
    else:
        fshapes = [jax.ShapeDtypeStruct((half, D), BF16), jax.ShapeDtypeStruct((half, D), F32)]
    return pl.pallas_call(
        functools.partial(attn_kernel, step, peer, chained),
        name="attn",
        grid_spec=pltpu.PrefetchScalarGridSpec(
            num_scalar_prefetch=1,
            grid=(1,),
            in_specs=[any_spec()] * 2 + [whole((QKV, D)), whole((OUT, D))] + [any_spec()] * (len(ins) - 5),
            out_specs=[any_spec()] * (5 + len(fshapes)),
            scratch_shapes=[
                pltpu.VMEM((SEQ, D), F32),
                pltpu.VMEM((SEQ, D), F32),
                pltpu.VMEM((SEQ, D), BF16),
                pltpu.VMEM((SEQ, D), BF16),
                pltpu.VMEM((QKV, SEQ), BF16),
                pltpu.VMEM((QKV, SEQ), BF16),
                pltpu.VMEM((OUT, SEQ), BF16),
                pltpu.VMEM((OUT, SEQ), BF16),
                pltpu.VMEM((SEQ, HEAD), BF16),
                pltpu.VMEM((SEQ, HEAD), BF16),
                pltpu.VMEM((SEQ, HEAD), F32),
                pltpu.VMEM((SEQ, HEAD), F32),
                pltpu.VMEM((SEQ, D), BF16 if peer else F32),
                pltpu.VMEM((QKV, D), F32),
                pltpu.VMEM((OUT, D), F32),
                pltpu.SemaphoreType.DMA((2, PARTS)),
                pltpu.SemaphoreType.DMA((2,)),
                pltpu.SemaphoreType.DMA((3,)),
                pltpu.SemaphoreType.DMA((2,)),
            ]
            + ([] if peer else [pltpu.VMEM((SEQ, D), BF16), pltpu.SemaphoreType.DMA((1,))]),
        ),
        out_shape=[
            full,
            full,
            jax.ShapeDtypeStruct((QKV, D), F32),
            jax.ShapeDtypeStruct((OUT, D), F32),
            jax.ShapeDtypeStruct((OUT, 2 * SEQ), BF16),
        ]
        + fshapes,
        input_output_aliases=alias,
        compiler_params=params(dimension_semantics=("arbitrary",)),
        cost_estimate=cost(15e9, 30e6),
    )(*ins)


def out_proj_kernel(chained, pos, y1, *refs):
    os_, ws = refs[:8], refs[8:16]
    refs = refs[18:] if chained else refs[17:]
    x1, oT, wo, sems = refs

    @pl.when(pl.program_id(0) == 0)
    def _():
        cps = []
        for k in range(8):
            at = pl.multiple_of(pos[k] * OUT, OUT)
            cps.append(pltpu.make_async_copy(os_[k], oT.at[pl.ds(at, OUT), :], sems.at[0, k]))
            cps.append(pltpu.make_async_copy(ws[k], wo.at[pl.ds(at, OUT), :], sems.at[1, k]))
        for cp in cps:
            cp.start()
        for cp in cps:
            cp.wait()

    col = pl.multiple_of(pl.program_id(0) * ROWS, ROWS)
    x1[...] = y1[...] - dot(oT[:, pl.ds(col, ROWS)], wo[...], TN)


def out_proj(step, pos, y1, os_, ws, dep, chain):
    per = SEQ // ROWS
    chained = chain is not None
    row = pl.BlockSpec((ROWS, D), lambda i, pos: ((i // per) * (STEPS * per) + step * per + i % per, 0))
    return pl.pallas_call(
        functools.partial(out_proj_kernel, chained),
        name="out_proj",
        grid_spec=pltpu.PrefetchScalarGridSpec(
            num_scalar_prefetch=1,
            grid=(2 * per,),
            in_specs=[row] + [any_spec()] * (18 if chained else 17),
            out_specs=row,
            scratch_shapes=[
                pltpu.VMEM((8 * OUT, 2 * SEQ), BF16),
                pltpu.VMEM((8 * OUT, D), BF16),
                pltpu.SemaphoreType.DMA((2, 8)),
            ],
        ),
        out_shape=jax.ShapeDtypeStruct((2 * STEPS * SEQ, D), F32),
        input_output_aliases={19: 0} if chained else {},
        compiler_params=params(dimension_semantics=("arbitrary",)),
        cost_estimate=cost(2 * 2 * SEQ * D * D, 30e6),
    )(pos, y1, *os_, *ws, dep, *([chain] if chained else []))


def norm_back_kernel(steps, chained, base, *refs):
    n = len(steps)
    xs, fs, c2 = refs[: 2 * n], refs[2 * n : 10 * n], refs[10 * n]
    refs = refs[10 * n + (3 if chained else 2) :]
    out, f, sems = refs
    per = SEQ // ROWS
    i = pl.program_id(0)
    size = SEQ // 4

    def copies(k):
        return [
            pltpu.make_async_copy(fs[8 * k + j], f.at[k, pl.ds(pl.multiple_of(base[2 + j] * size, size), size), :], sems.at[k, j])
            for j in range(8)
        ]

    @pl.when(i == 0)
    def _():
        for k in range(n):
            for cp in copies(k):
                cp.start()

    for k in range(n):
        @pl.when(i == 2 * per * k)
        def _():
            for cp in copies(k):
                cp.wait()

    def run(k, seq, x_ref):
        owner = base[0] if seq == 0 else 1 - base[0]
        at0 = owner * SEQ + (i - (2 * k + seq) * per) * ROWS

        def rows(r, _):
            at = pl.ds(pl.multiple_of(r * 16, 16), 16)
            x = x_ref[at, :]
            q = inv_rms(x)
            nf = x * q
            g = f[k, pl.ds(pl.multiple_of(at0 + r * 16, 16), 16), :].astype(F32)
            out[at, :] = c2[at, :] + q * (g - nf * jnp.mean(nf * g, axis=-1, keepdims=True))
            return 0

        lax.fori_loop(0, ROWS // 16, rows, 0, unroll=4)

    for k in range(n):
        for seq in range(2):
            @pl.when(i // per == 2 * k + seq)
            def _():
                run(k, seq, xs[2 * k + seq])


def norm_back(steps, core, xs, fs, c2, dep, chain):
    per = SEQ // ROWS
    n = len(steps)
    chained = chain is not None

    def xspec(j):
        return pl.BlockSpec((ROWS, D), lambda i, base: (jnp.clip(i - j * per, 0, per - 1), 0))

    def at(i, base):
        owner = jnp.where((i // per) % 2 == 0, base[0], 1 - base[0])
        return (owner * (STEPS * per) + (steps[0] + i // (2 * per)) * per + i % per, 0)

    row = pl.BlockSpec((ROWS, D), at)
    return pl.pallas_call(
        functools.partial(norm_back_kernel, steps, chained),
        name="norm_back",
        grid_spec=pltpu.PrefetchScalarGridSpec(
            num_scalar_prefetch=1,
            grid=(2 * per * n,),
            in_specs=[xspec(j) for j in range(2 * n)] + [any_spec()] * (8 * n) + [row, any_spec()] + [any_spec()] * (1 if chained else 0),
            out_specs=row,
            scratch_shapes=[pltpu.VMEM((n, 2 * SEQ, D), BF16), pltpu.SemaphoreType.DMA((n, 8))],
        ),
        out_shape=jax.ShapeDtypeStruct((2 * STEPS * SEQ, D), F32),
        input_output_aliases={10 * n + 3: 0} if chained else {},
        compiler_params=params(dimension_semantics=("arbitrary",)),
        cost_estimate=cost(n * 4e9, n * 40e6),
    )(core, *xs, *fs, c2, dep, *([chain] if chained else []))


def solution(mesh):
    act_spec = P("dp", None, None)
    weight_specs = (P(None, None, "tp", None, None), P(None, "tp", None, None), P(None, None, "tp"), P(None, "tp", None))
    grad_specs = (P("dp", None, "tp", None, None), P("dp", "tp", None, None), P("dp", None, "tp"), P("dp", "tp", None))

    pairs = {
        "core": [(t, t ^ 1) for t in range(8)],
        "a": [(t, t ^ (4 if t & 1 else 2)) for t in range(8)],
        "b": [(t, t ^ (2 if t & 1 else 4)) for t in range(8)],
    }

    def swap(x, kind):
        return lax.ppermute(x, "tp", pairs[kind])

    def local_backward(out_y1, out_y2, cot_y1, cot_y2, w_qkv, w_out, w_up, w_down):
        rank = lax.axis_index("tp")
        core = rank & 1

        def near(r):
            return jnp.where(r & 1 == 0, (r >> 1) & 1, (r >> 2) & 1)

        def far(r):
            return jnp.where(r & 1 == 0, (r >> 2) & 1, (r >> 1) & 1)

        mask_a = jnp.where(core == 0, 2, 4)
        mask_b = jnp.where(core == 0, 4, 2)
        slots = [rank, rank ^ mask_a, rank ^ mask_b, rank ^ 6, rank ^ 1, rank ^ 1 ^ mask_b, rank ^ 1 ^ mask_a, rank ^ 7]
        pos = jnp.stack(slots).astype(jnp.int32)
        base = jnp.stack([core, near(rank)] + [(r & 1) * 4 + near(r) * 2 + far(r) for r in slots]).astype(jnp.int32)
        far_bit = far(rank)
        flat = lambda z: z.reshape(2 * STEPS * SEQ, D)
        y1, y2, c1, c2 = flat(out_y1), flat(out_y2), flat(cot_y1), flat(cot_y2)
        w1, w2 = w_up[0], w_down[0]
        wq = jnp.transpose(w_qkv[0], (1, 2, 3, 0)).reshape(QKV, D)
        wo = w_out[0].reshape(OUT, D)

        w1p, w2p = swap(w1, "core"), swap(w2, "core")
        w1a, w2a = swap(w1, "a"), swap(w2, "a")
        w1b, w2b = swap(w1, "b"), swap(w2, "b")
        n_all, cot_all, act, dh, gp, np_ = mlp_own(base, y1, c2, w1, w1p, w2, w2p)
        g1o, g1p = mlp_grad(False, n_all, dh, np_)
        w1a, w2a, w1b, w2b, wo, g1o = lax.optimization_barrier((w1a, w2a, w1b, w2b, wo, g1o))
        w1d, w2d = swap(w1b, "a"), swap(w2b, "a")
        rest_ab = [w1a, swap(w1a, "core"), w2a, swap(w2a, "core")]
        rest_ab += [w1b, swap(w1b, "core"), w2b, swap(w2b, "core")]
        g1r = swap(g1p, "core")
        g2o, g2p = mlp_grad(True, act, cot_all, g1o)
        g2r = swap(g2p, "core")
        common = (base, n_all, cot_all, y1, y2, c1, gp, np_)
        part = mlp_rest(0, *common, rest_ab, None, g2o, False)
        rest_d = [w1d, swap(w1d, "core"), w2d, swap(w2d, "core")]
        g_up = g1o + g1r
        g_down = g2o + g2r
        wos = [wo, swap(wo, "a"), swap(wo, "b")]
        wos.append(swap(wos[2], "a"))
        wos += [swap(w, "core") for w in wos]

        x2s, d1s = [None] * STEPS, [None] * STEPS
        ots, fns = [None] * STEPS, [None] * STEPS
        chain = x1 = dx2 = None
        fn_peer = oT_half = None

        def rest(s, dep):
            if s == 0:
                x, d = mlp_rest(0, *common, rest_d, part, dep, True)
            else:
                x, d = mlp_rest(s, *common, rest_ab + rest_d, None, dep, True)
            x2s[s], d1s[s] = (x, swap(x, "core")), (d, swap(d, "core"))
            return x

        def peer(s, dep):
            nonlocal chain, fn_peer, oT_half
            *chain, oT_half, fn = attn(s, True, base, x2s[s][1], d1s[s][1], wq, wo, None, None, dep, chain)
            fn_peer = swap(fn, "core")
            return fn

        def own(s, dep):
            nonlocal chain
            *chain, oT, go, stay = attn(s, False, base, x2s[s][0], d1s[s][0], wq, wo, fn_peer, oT_half, dep, chain)
            items = [oT, swap(oT, "a"), swap(oT, "b")]
            items.append(swap(items[2], "a"))
            ots[s] = items + [swap(o, "core") for o in items]
            got = swap(go, "a").reshape(2, SEQ // 4, D)
            stay = stay.reshape(2, SEQ // 4, D)
            pick = lambda z, k: lax.dynamic_index_in_dim(z, k, 0, keepdims=False)
            send = (pick(stay, 1 - far_bit) + pick(got, 1 - far_bit).astype(F32)).astype(BF16)
            got2 = swap(send, "b")
            quarter = (pick(stay, far_bit) + pick(got, far_bit).astype(F32) + got2.astype(F32)).astype(BF16)
            pieces = [quarter, swap(quarter, "a"), swap(quarter, "b")]
            pieces.append(swap(pieces[2], "a"))
            fns[s] = pieces + [swap(z, "core") for z in pieces]
            return go

        def proj(s, dep):
            nonlocal x1
            x1 = out_proj(s, pos, y1, ots[s], wos, y1 if dep is x1 else dep, x1)
            return x1

        def back(steps, dep):
            nonlocal dx2
            xs = [x for s in steps for x in x2s[s]]
            fs = [f for s in steps for f in fns[s]]
            dx2 = norm_back(steps, base, xs, fs, c2, c2 if dep is dx2 else dep, dx2)
            return dx2

        t = rest(0, part[0])
        for call in (
            (rest, 1), (peer, 0), (rest, 2), (own, 0), (peer, 1), (rest, 3), (own, 1), (peer, 2), (proj, 0), (own, 2),
            (peer, 3), (proj, 1), (own, 3), (back, (0, 1)), (proj, 2), (proj, 3), (back, (2,)), (back, (3,)),
        ):
            t = call[0](call[1], t)

        x2, dx1, aq, ao = chain
        full = lambda z: z.reshape(2 * STEPS, SEQ, D)
        g_qkv = jnp.transpose(aq.reshape(HEADS_DEV, 3, HEAD, D), (3, 0, 1, 2))
        g_out = ao.reshape(HEADS_DEV, HEAD, D)
        return full(x1), full(x2), full(dx1), full(dx2), g_qkv[None], g_out[None], g_up[None], g_down[None]

    return jax.shard_map(
        local_backward,
        mesh=mesh,
        in_specs=(act_spec,) * 4 + weight_specs,
        out_specs=(act_spec,) * 4 + grad_specs,
        check_vma=False,
    )
```

time: 838 us -> 908 us (1.084)
  starting transfers between devices: 14 us -> 51.6 us
  Pallas kernels: 663 us -> 685 us
  between operations: 14.6 us -> 1.87 us
  other arithmetic: 8.17 us -> 17.7 us
    ppermute x24 -> x99, waiting for transfers between devices: 25.2 us -> 136 us  [swap(): return lax.ppermute(x, 'tp', pairs[kind])]
    psum x4 -> x0, waiting for transfers between devices: 89.1 us -> none  [att(): fns[s] = lax.psum(fn.reshape(2 * SEQ, D), 'tp')]
    ppermute x24 -> x99, starting transfers between devices: 13.4 us -> 51.6 us  [swap(): return lax.ppermute(x, 'tp', pairs[kind])]
    all_gather x5 -> x0, waiting for transfers between devices: 15.8 us -> none  [the longest x4 15.8 us: att(): ots[s] = lax.all_gather(oT, 'tp', axis=0, tiled=True)]
    pallas_call x2, Pallas kernels: 41 us -> 54 us  [mlp_grad(): pl.pallas_call(functools.partial(grad_kernel, split_rows), name='mlp_grad...]
    convert_element_type x0 -> x8, other arithmetic: none -> 9.58 us  [the longest x4 5.06 us: own(): (pick(stay, 1 - far_bit) + pick(got, 1 - far_bit).astype(F32)).astype(BF16)]
    pallas_call x16 -> x20, Pallas kernels: 556 us -> 564 us  [the longest x5 253 us: mlp_rest(): pl.pallas_call(functools.partial(mlp_rest_kernel, step, chunks, resumed,...]
  transfers between devices with their start and end apart: 33 -> 99, of which waited for: 9 -> 19; matrix products, arithmetic and copies ran while one was open for 1% -> 2% of each run, Pallas kernels for 70% -> 71%
where the time goes in v2:
time: 908 us; the launch traced here: 899 us
  Pallas kernels  685 us (75%)
  waiting for transfers between devices  136 us (15%)
  starting transfers between devices  51.6 us (6%)
  other arithmetic  17.7 us (2%)
    pallas_call x5, Pallas kernels, mlp_rest(): pl.pallas_call(functools.partial(mlp_rest_kernel, step, chunks, resumed,...  253 us
    pallas_call x8, Pallas kernels, attn(): pl.pallas_call(functools.partial(attn_kernel, step, peer, chained), name=...  176 us
    ppermute x99, waiting for transfers between devices, swap(): return lax.ppermute(x, 'tp', pairs[kind])  136 us
    pallas_call x3, Pallas kernels, norm_back(): pl.pallas_call(functools.partial(norm_back_kernel, steps, chained), name=...  68.6 us
    pallas_call x1, Pallas kernels, mlp_own(): pl.pallas_call(mlp_own_kernel, name='mlp_own', grid_spec=pltpu.PrefetchSc...  67.8 us
    pallas_call x4, Pallas kernels, out_proj(): pl.pallas_call(functools.partial(out_proj_kernel, chained), name='out_pro...  66.2 us
    pallas_call x2, Pallas kernels, mlp_grad(): pl.pallas_call(functools.partial(grad_kernel, split_rows), name='mlp_grad...  54 us
    ppermute x99, starting transfers between devices, swap(): return lax.ppermute(x, 'tp', pairs[kind])  51.6 us
  transfers between devices with their start and end apart: 99, of which 19 were waited for; matrix products, arithmetic and copies ran while one was open for 2% of the time, Pallas kernels for 71%

profile of v2, /device:TPU:0, one launch (start us, length us, event | category | flops | bytes accessed | tf_op | source)
XLA Modules:
  0.0 899.1 jit_solution(17146081819978453431)
XLA Ops:
  1.4 2.9 collective-permute-start.2
  4.4 2.0 collective-permute-start.4
  7.7 67.8 %mlp_own.1 = (bf16[4096,1280]{1,0:T(8,128)(2,1)}, bf16[4096,1280]{1,0:T(8,128)(2,1)}, bf16[4096,1280]{1,0:T(8,128)(2,1)}, bf16[4096,1280]{1,0:T(8,128)(2,1)}, f3...) custom-call(s32[10]{0:T(128)} %stack.79.base, f32[8192,1280]{1,0:T(8,128)} %bitcast.76, f32[8192,1280]{1,0:T(8,128)} %bitcast.100, ...), custom_call_target="tpu_custom_call" | custom-call | flops 53687091200 | bytes 120000000 | tf_op jit(solution)/shard_map/mlp_own/pallas_call | solution.py:94
  75.5 20.3 %mlp_grad.2 = (f32[1280,640]{1,0:T(8,128)}, f32[1280,640]{1,0:T(8,128)}) custom-call(bf16[4096,1280]{1,0:T(8,128)(2,1)} %get-tuple-element.86.a.n_in, bf16[4096,1280]{1,0:T(8,128)(2,1)} %get-tuple-element.90.b, f32[4096,1280]{1,0:T(8,128)} %get-tuple-element.89.dep.np_), custom_call_target="tpu_custom_call" | custom-call | flops 13421772800 | bytes 30000000 | tf_op jit(solution)/shard_map/mlp_grad/pallas_call | solution.py:137
  96.4 2.3 collective-permute-start.10
  100.7 33.7 %mlp_grad.3 = (f32[640,1280]{1,0:T(8,128)}, f32[640,1280]{1,0:T(8,128)}) custom-call(bf16[4096,1280]{1,0:T(8,128)(2,1)} %get-tuple-element.96.a, bf16[4096,1280]{1,0:T(8,128)(2,1)} %get-tuple-element.87.b.cot_in, f32[1280,640]{1,0:T(8,128)} %get-tuple-element.97.dep), custom_call_target="tpu_custom_call" | custom-call | flops 13421772800 | bytes 30000000 | tf_op jit(solution)/shard_map/mlp_grad/pallas_call | solution.py:137
  135.7 36.3 %mlp_rest.5 = (f32[1024,1280]{1,0:T(8,128)}, f32[1024,1280]{1,0:T(8,128)}) custom-call(s32[10]{0:T(128)} %stack.79.base, bf16[4096,1280]{1,0:T(8,128)(2,1)} %get-tuple-element.86.a.n_in, bf16[4096,1280]{1,0:T(8,128)(2,1)} %get-tuple-element.87.b.cot_in, f32[8192,1280]{1,0:T(8,128)} %bitcast.77, f32[8192,1280]{1,0:T(8,128)} %bitcast.90, ...), custom_call_target="tpu_custom_call" | custom-call | flops 26843545600 | bytes 60000000 | tf_op jit(solution)/shard_map/mlp_rest/pallas_call | solution.py:240
  173.2 30.8 %mlp_rest.6 = (f32[1024,1280]{1,0:T(8,128)}, f32[1024,1280]{1,0:T(8,128)}) custom-call(s32[10]{0:T(128)} %stack.79.base, bf16[4096,1280]{1,0:T(8,128)(2,1)} %get-tuple-element.86.a.n_in, bf16[4096,1280]{1,0:T(8,128)(2,1)} %get-tuple-element.87.b.cot_in, f32[8192,1280]{1,0:T(8,128)} %bitcast.78, f32[8192,1280]{1,0:T(8,128)} %bitcast.91, ...), custom_call_target="tpu_custom_call" | custom-call | flops 13421772800 | bytes 60000000 | tf_op jit(solution)/shard_map/mlp_rest/pallas_call | solution.py:240
  204.7 2.0 collective-permute-start.33
  208.1 61.9 %mlp_rest.7 = (f32[1024,1280]{1,0:T(8,128)}, f32[1024,1280]{1,0:T(8,128)}) custom-call(s32[10]{0:T(128)} %stack.79.base, bf16[4096,1280]{1,0:T(8,128)(2,1)} %get-tuple-element.86.a.n_in, bf16[4096,1280]{1,0:T(8,128)(2,1)} %get-tuple-element.87.b.cot_in, f32[8192,1280]{1,0:T(8,128)} %bitcast.79, f32[8192,1280]{1,0:T(8,128)} %bitcast.92, ...), custom_call_target="tpu_custom_call" | custom-call | flops 40265318400 | bytes 60000000 | tf_op jit(solution)/shard_map/mlp_rest/pallas_call | solution.py:240
  270.7 21.2 %attn.8 = (f32[8192,1280]{1,0:T(8,128)}, f32[8192,1280]{1,0:T(8,128)}, f32[480,1280]{1,0:T(8,128)}, f32[160,1280]{1,0:T(8,128)}, bf16[160,2048]{1,0:T(8,128)(2,1)}, /*index=5*/bf16[1024,1280]{1,0:T(8,128)(2,1)}) custom-call(s32[10]{0:T(128)} %stack.79.base, f32[1024,1280]{1,0:T(8,128)} %collective-permute-done.16.x2.refs_1_, ...), custom_call_target="tpu_custom_call" | custom-call | flops 15000000512 | bytes 30000000 | tf_op jit(solution)/shard_map/attn/pallas_call | solution.py:403
  292.0 62.1 %mlp_rest.8 = (f32[1024,1280]{1,0:T(8,128)}, f32[1024,1280]{1,0:T(8,128)}) custom-call(s32[10]{0:T(128)} %stack.79.base, bf16[4096,1280]{1,0:T(8,128)(2,1)} %get-tuple-element.86.a.n_in, bf16[4096,1280]{1,0:T(8,128)(2,1)} %get-tuple-element.87.b.cot_in, f32[8192,1280]{1,0:T(8,128)} %bitcast.80, f32[8192,1280]{1,0:T(8,128)} %bitcast.93, ...), custom_call_target="tpu_custom_call" | custom-call | flops 40265318400 | bytes 60000000 | tf_op jit(solution)/shard_map/mlp_rest/pallas_call | solution.py:240
  355.1 22.1 %attn.9 = (f32[8192,1280]{1,0:T(8,128)}, f32[8192,1280]{1,0:T(8,128)}, f32[480,1280]{1,0:T(8,128)}, f32[160,1280]{1,0:T(8,128)}, bf16[160,2048]{1,0:T(8,128)(2,1...) custom-call(s32[10]{0:T(128)} %stack.79.base, ...), custom_call_target="tpu_custom_call", output_to_operand_aliasing={{0}: (7, {}), {1}: (8, {}), {2}: (9, {}), {3}: (10, {}), {4... | custom-call | flops 15000000512 | bytes 30000000 | tf_op jit(solution)/shard_map/attn/pallas_call | solution.py:403
  377.8 21.8 %attn.10 = (f32[8192,1280]{1,0:T(8,128)}, f32[8192,1280]{1,0:T(8,128)}, f32[480,1280]{1,0:T(8,128)}, f32[160,1280]{1,0:T(8,128)}, bf16[160,2048]{1,0:T(8,128)(2,1)}, /*index=5*/bf16[1024,1280]{1,0:T(8,128)(2,1)}) custom-call(s32[10]{0:T(128)} %stack.79.base, ...), custom_call_target="tpu_custom_call", output_to_operand_aliasing={{0}: (5, {}), {1}: (6, {}), {2}: (7, {}), {3}: (8, {})} | custom-call | flops 15000000512 | bytes 30000000 | tf_op jit(solution)/shard_map/attn/pallas_call | solution.py:403
  400.3 61.9 %mlp_rest.9 = (f32[1024,1280]{1,0:T(8,128)}, f32[1024,1280]{1,0:T(8,128)}) custom-call(s32[10]{0:T(128)} %stack.79.base, bf16[4096,1280]{1,0:T(8,128)(2,1)} %get-tuple-element.86.a.n_in, bf16[4096,1280]{1,0:T(8,128)(2,1)} %get-tuple-element.87.b.cot_in, f32[8192,1280]{1,0:T(8,128)} %bitcast.81, f32[8192,1280]{1,0:T(8,128)} %bitcast.94, ...), custom_call_target="tpu_custom_call" | custom-call | flops 40265318400 | bytes 60000000 | tf_op jit(solution)/shard_map/mlp_rest/pallas_call | solution.py:240
  464.8 22.0 %attn.11 = (f32[8192,1280]{1,0:T(8,128)}, f32[8192,1280]{1,0:T(8,128)}, f32[480,1280]{1,0:T(8,128)}, f32[160,1280]{1,0:T(8,128)}, bf16[160,2048]{1,0:T(8,128)(2,...) custom-call(s32[10]{0:T(128)} %stack.79.base, ...), custom_call_target="tpu_custom_call", output_to_operand_aliasing={{0}: (7, {}), {1}: (8, {}), {2}: (9, {}), {3}: (10, {}), {4... | custom-call | flops 15000000512 | bytes 30000000 | tf_op jit(solution)/shard_map/attn/pallas_call | solution.py:403
  489.4 22.2 %attn.12 = (f32[8192,1280]{1,0:T(8,128)}, f32[8192,1280]{1,0:T(8,128)}, f32[480,1280]{1,0:T(8,128)}, f32[160,1280]{1,0:T(8,128)}, bf16[160,2048]{1,0:T(8,128)(2,1)}, /*index=5*/bf16[1024,1280]{1,0:T(8,128)(2,1)}) custom-call(s32[10]{0:T(128)} %stack.79.base, ...), custom_call_target="tpu_custom_call", output_to_operand_aliasing={{0}: (5, {}), {1}: (6, {}), {2}: (7, {}), {3}: (8, {})} | custom-call | flops 15000000512 | bytes 30000000 | tf_op jit(solution)/shard_map/attn/pallas_call | solution.py:403
  513.9 3.8 collective-permute-done.29.refs_5_
  519.3 9.0 %collective-permute-done.62 = bf16[256,1280]{1,0:T(8,128)(2,1)S(1)} collective-permute-done((bf16[256,1280]{1,0:T(8,128)(2,1)S(1)}, bf16[256,1280]{1,0:T(8,128)(2,1)S(1)}, u32[]{:S(2)}, u32[]{:S(2)}) %collective-permute-start.62) | collective-permute-done | bytes 655392 | tf_op jit(solution)/shard_map/ppermute | solution.py:585
  532.1 16.4 %out_proj.4.refs_6_.refs_17_ = f32[8192,1280]{1,0:T(8,128)} custom-call(s32[8]{0:T(128)} %stack.68.pos, f32[8192,1280]{1,0:T(8,128)} %bitcast.82, bf16[160,2048]{1,0:T(8,128)(2,1)} %get-tuple-element.138.refs_0_, bf16[160,2048]{1,0:T(8,128)(2,1)} %collective-permute-done.25.refs_1_, bf16[160,2048]{1,0:T(8,128)(2,1)} %collective-permute-done.26.refs_2_, ...), custom_call_target="tpu_custom_call" | custom-call | flops 6710886400 | bytes 30000000 | tf_op jit(solution)/shard_map/out_proj/pallas_call | solution.py:473
  550.0 22.3 %attn.13 = (f32[8192,1280]{1,0:T(8,128)}, f32[8192,1280]{1,0:T(8,128)}, f32[480,1280]{1,0:T(8,128)}, f32[160,1280]{1,0:T(8,128)}, bf16[160,2048]{1,0:T(8,128)(2,...) custom-call(s32[10]{0:T(128)} %stack.79.base, ...), custom_call_target="tpu_custom_call", output_to_operand_aliasing={{0}: (7, {}), {1}: (8, {}), {2}: (9, {}), {3}: (10, {}), {4... | custom-call | flops 15000000512 | bytes 30000000 | tf_op jit(solution)/shard_map/attn/pallas_call | solution.py:403
  574.9 22.0 %attn.14 = (f32[8192,1280]{1,0:T(8,128)}, f32[8192,1280]{1,0:T(8,128)}, f32[480,1280]{1,0:T(8,128)}, f32[160,1280]{1,0:T(8,128)}, bf16[160,2048]{1,0:T(8,128)(2,1)}, /*index=5*/bf16[1024,1280]{1,0:T(8,128)(2,1)}) custom-call(s32[10]{0:T(128)} %stack.79.base, ...), custom_call_target="tpu_custom_call", output_to_operand_aliasing={{0}: (5, {}), {1}: (6, {}), {2}: (7, {}), {3}: (8, {})} | custom-call | flops 15000000512 | bytes 30000000 | tf_op jit(solution)/shard_map/attn/pallas_call | solution.py:403
  599.3 4.8 collective-permute-done.70
  606.2 4.7 collective-permute-done.40.refs_1_
  611.5 6.6 collective-permute-done.65.refs_7_
  618.7 12.0 %collective-permute-done.42.refs_3_ = bf16[160,2048]{1,0:T(8,128)(2,1)S(1)} collective-permute-done((bf16[160,2048]{1,0:T(8,128)(2,1)S(1)}, bf16[160,2048]{1,0:T(8,128)(2,1)S(1)}, u32[]{:S(2)}, u32[]{:S(2)}) %collective-permute-start.42) | collective-permute-done | bytes 655392 | tf_op jit(solution)/shard_map/ppermute | solution.py:585
  635.2 16.9 %out_proj.5.refs_6_.refs_17_ = f32[8192,1280]{1,0:T(8,128)} custom-call(s32[8]{0:T(128)} %stack.68.pos, f32[8192,1280]{1,0:T(8,128)} %bitcast.83, bf16[160,2048]{1,0:T(8,128)(2,1)} %get-tuple-element.150.refs_0_, bf16[160,2048]{1,0:T(8,128)(2,1)} %copy-done.26, bf16[160,2048]{1,0:T(8,128)(2,1)} %copy-done.25, ...), custom_call_target="tpu_custom_call", output_to_operand_aliasing={{}: (19, {})} | custom-call | flops 6710886400 | bytes 30000000 | tf_op jit(solution)/shard_map/out_proj/pallas_call | solution.py:473
  654.5 1.7 collective-permute-start.55
  656.3 22.1 %attn.15 = (f32[8192,1280]{1,0:T(8,128)}, f32[8192,1280]{1,0:T(8,128)}, f32[480,1280]{1,0:T(8,128)}, f32[160,1280]{1,0:T(8,128)}, bf16[160,2048]{1,0:T(8,128)(2,...) custom-call(s32[10]{0:T(128)} %stack.79.base, ...), custom_call_target="tpu_custom_call", output_to_operand_aliasing={{0}: (7, {}), {1}: (8, {}), {2}: (9, {}), {3}: (10, {}), {4... | custom-call | flops 15000000512 | bytes 30000000 | tf_op jit(solution)/shard_map/attn/pallas_call | solution.py:403
  678.8 11.5 %collective-permute-done.88 = bf16[512,1280]{1,0:T(8,128)(2,1)} collective-permute-done((bf16[512,1280]{1,0:T(8,128)(2,1)}, bf16[512,1280]{1,0:T(8,128)(2,1)}, u32[]{:S(2)}, u32[]{:S(2)}) %collective-permute-start.88) | collective-permute-done | bytes 1310752 | tf_op jit(solution)/shard_map/ppermute | solution.py:585
  690.7 1.7 fusion.7
  694.5 3.7 collective-permute-done.54.refs_1_
  698.4 26.9 %collective-permute-done.74.refs_15_ = bf16[256,1280]{1,0:T(8,128)(2,1)S(1)} collective-permute-done((bf16[256,1280]{1,0:T(8,128)(2,1)S(1)}, bf16[256,1280]{1,0:T(8,128)(2,1)S(1)}, u32[]{:S(2)}, u32[]{:S(2)}) %collective-permute-start.74) | collective-permute-done | bytes 655392 | tf_op jit(solution)/shard_map/ppermute | solution.py:585
  727.5 4.9 collective-permute-done.56.refs_3_
  733.4 1.7 collective-permute-start.80
  736.4 13.6 %collective-permute-done.91.refs_4_ = bf16[256,1280]{1,0:T(8,128)(2,1)S(1)} collective-permute-done((bf16[256,1280]{1,0:T(8,128)(2,1)S(1)}, bf16[256,1280]{1,0:T(8,128)(2,1)S(1)}, u32[]{:S(2)}, u32[]{:S(2)}) %collective-permute-start.91) | collective-permute-done | bytes 655392 | tf_op jit(solution)/shard_map/ppermute | solution.py:585
  750.1 14.0 %collective-permute-done.80 = bf16[256,1280]{1,0:T(8,128)(2,1)S(1)} collective-permute-done((bf16[256,1280]{1,0:T(8,128)(2,1)S(1)}, bf16[256,1280]{1,0:T(8,128)(2,1)S(1)}, u32[]{:S(2)}, u32[]{:S(2)}) %collective-permute-start.80) | collective-permute-done | bytes 655392 | tf_op jit(solution)/shard_map/ppermute | solution.py:585
  764.2 4.1 add_bitcast_fusion
  769.1 2.9 collective-permute-done.48.refs_2_
  773.6 4.1 add_bitcast_fusion.1
  777.7 5.3 collective-permute-done.92.refs_5_
  783.5 9.7 %collective-permute-done.49.refs_3_ = bf16[160,2048]{1,0:T(8,128)(2,1)} collective-permute-done((bf16[160,2048]{1,0:T(8,128)(2,1)}, bf16[160,2048]{1,0:T(8,128)(2,1)}, u32[]{:S(2)}, u32[]{:S(2)}) %collective-permute-start.49) | collective-permute-done | bytes 655392 | tf_op jit(solution)/shard_map/ppermute | solution.py:585
  793.4 1.9 collective-permute-start.83
  795.3 32.4 %norm_back.3.refs_16_.refs_12_ = f32[8192,1280]{1,0:T(8,128)} custom-call(s32[10]{0:T(128)} %stack.79.base, f32[1024,1280]{1,0:T(8,128)} %get-tuple-element.101.refs_12_.x2.refs_0_, f32[1024,1280]{1,0:T(8,128)} %collective-permute-done.16.x2.refs_1_, f32[1024,1280]{1,0:T(8,128)} %get-tuple-element.102.refs_0_.x2.refs_2_, ...), custom_call_target="tpu_custom_call" | custom-call | flops 8000000000 | bytes 80000000 | tf_op jit(solution)/shard_map/norm_back/pallas_call | solution.py:556
  827.8 16.5 %out_proj.6.refs_17_ = f32[8192,1280]{1,0:T(8,128)} custom-call(s32[8]{0:T(128)} %stack.68.pos, f32[8192,1280]{1,0:T(8,128)} %bitcast.84, bf16[160,2048]{1,0:T(8,128)(2,1)} %get-tuple-element.152.refs_0_, bf16[160,2048]{1,0:T(8,128)(2,1)} %copy-done.35, bf16[160,2048]{1,0:T(8,128)(2,1)} %collective-permute-done.55.refs_2_, ...), custom_call_target="tpu_custom_call", output_to_operand_aliasing={{}: (19, {})} | custom-call | flops 6710886400 | bytes 30000000 | tf_op jit(solution)/shard_map/out_proj/pallas_call | solution.py:473
  845.4 16.4 %out_proj.7.refs_11_ = f32[8192,1280]{1,0:T(8,128)} custom-call(s32[8]{0:T(128)} %stack.68.pos, f32[8192,1280]{1,0:T(8,128)} %bitcast.85, bf16[160,2048]{1,0:T(8,128)(2,1)} %get-tuple-element.151.refs_0_, bf16[160,2048]{1,0:T(8,128)(2,1)} %collective-permute-done.47.refs_1_, ...), custom_call_target="tpu_custom_call", output_to_operand_aliasing={{}: (19, {})} | custom-call | flops 6710886400 | bytes 30000000 | tf_op jit(solution)/shard_map/out_proj/pallas_call | solution.py:473
  861.8 18.1 %norm_back.4.refs_12_ = f32[8192,1280]{1,0:T(8,128)} custom-call(s32[10]{0:T(128)} %stack.79.base, f32[1024,1280]{1,0:T(8,128)} %get-tuple-element.112.refs_6_.x2.refs_0_, f32[1024,1280]{1,0:T(8,128)} %collective-permute-done.21.x2.refs_1_, bf16[256,1280]{1,0:T(8,128)(2,1)} %copy-done.16, ...), custom_call_target="tpu_custom_call", output_to_operand_aliasing={{}: (13, {})} | custom-call | flops 4000000000 | bytes 40000000 | tf_op jit(solution)/shard_map/norm_back/pallas_call | solution.py:556
  880.8 18.1 %norm_back.5 = f32[8192,1280]{1,0:T(8,128)} custom-call(s32[10]{0:T(128)} %stack.79.base, f32[1024,1280]{1,0:T(8,128)} %get-tuple-element.119.refs_6_.x2.refs_0_, f32[1024,1280]{1,0:T(8,128)} %collective-permute-done.19.x2.refs_1_, bf16[256,1280]{1,0:T(8,128)(2,1)} %copy-done.17, ...), custom_call_target="tpu_custom_call", output_to_operand_aliasing={{}: (13, {})} | custom-call | flops 4000000000 | bytes 40000000 | tf_op jit(solution)/shard_map/norm_back/pallas_call | solution.py:556
  (283 shorter events, 53.9 us)
Async XLA Ops:
  1.4 94.4 %collective-permute-start.2 = (bf16[1280,640]{1,0:T(8,128)(2,1)}, bf16[1280,640]{1,0:T(8,128)(2,1)S(1)}, u32[]{:S(2)}, u32[]{:S(2)}) collective-permute-start(bf16[1280,640]{1,0:T(8,128)(2,1)} %bitcast.127), channel_id=1, source_target_pairs={{0,2},{1,5},{2,0},{3,7},{4,6},{5,1},{6,4},{7,3},{8,10},{9,13},{10,... | collective-permute-start | bytes 4915208 | tf_op jit(solution)/shard_map/ppermute | solution.py:585
  4.4 91.4 %collective-permute-start.3 = (bf16[640,1280]{1,0:T(8,128)(2,1)}, bf16[640,1280]{1,0:T(8,128)(2,1)}, u32[]{:S(2)}, u32[]{:S(2)}) collective-permute-start(bf16[640,1280]{1,0:T(8,128)(2,1)} %bitcast.131), channel_id=1, source_target_pairs={{0,2},{1,5},{2,0},{3,7},{4,6},{5,1},{6,4},{7,3},{8,10},{9,13},{10,... | collective-permute-start | bytes 4915208 | tf_op jit(solution)/shard_map/ppermute | solution.py:585
  4.4 91.4 %collective-permute-start.4 = (bf16[1280,640]{1,0:T(8,128)(2,1)}, bf16[1280,640]{1,0:T(8,128)(2,1)}, u32[]{:S(2)}, u32[]{:S(2)}) collective-permute-start(bf16[1280,640]{1,0:T(8,128)(2,1)} %bitcast.128), channel_id=1, source_target_pairs={{0,4},{1,3},{2,6},{3,1},{4,0},{5,7},{6,2},{7,5},{8,12},{9,11},{10,... | collective-permute-start | bytes 4915208 | tf_op jit(solution)/shard_map/ppermute | solution.py:585
  7.1 88.7 %collective-permute-start.5 = (bf16[640,1280]{1,0:T(8,128)(2,1)}, bf16[640,1280]{1,0:T(8,128)(2,1)}, u32[]{:S(2)}, u32[]{:S(2)}) collective-permute-start(bf16[640,1280]{1,0:T(8,128)(2,1)} %bitcast.132), channel_id=1, source_target_pairs={{0,4},{1,3},{2,6},{3,1},{4,0},{5,7},{6,2},{7,5},{8,12},{9,11},{10,... | collective-permute-start | bytes 4915208 | tf_op jit(solution)/shard_map/ppermute | solution.py:585
  95.9 39.8 %collective-permute-start.8 = (bf16[1280,640]{1,0:T(8,128)(2,1)}, bf16[1280,640]{1,0:T(8,128)(2,1)}, u32[]{:S(2)}, u32[]{:S(2)}) collective-permute-start(bf16[1280,640]{1,0:T(8,128)(2,1)} %collective-permute-done.4.refs_4_), channel_id=1, source_target_pairs={{0,1},{1,0},{2,3},{3,2},{4,5},{5,4},{6,7},{7,6},{8,9},{9,8},{10,11... | collective-permute-start | bytes 4915208 | tf_op jit(solution)/shard_map/ppermute | solution.py:585
  96.4 38.0 %collective-permute-start.10 = (bf16[1280,640]{1,0:T(8,128)(2,1)}, bf16[1280,640]{1,0:T(8,128)(2,1)}, u32[]{:S(2)}, u32[]{:S(2)}) collective-permute-start(bf16[1280,640]{1,0:T(8,128)(2,1)} %collective-permute-done.4.refs_4_), channel_id=1, source_target_pairs={{0,2},{1,5},{2,0},{3,7},{4,6},{5,1},{6,4},{7,3},{8,10},{9,13},{10,... | collective-permute-start | bytes 4915208 | tf_op jit(solution)/shard_map/ppermute | solution.py:585
  98.7 37.0 %collective-permute-start.12 = (bf16[640,1280]{1,0:T(8,128)(2,1)}, bf16[640,1280]{1,0:T(8,128)(2,1)}, u32[]{:S(2)}, u32[]{:S(2)}) collective-permute-start(bf16[640,1280]{1,0:T(8,128)(2,1)} %collective-permute-done.5.refs_6_), channel_id=1, source_target_pairs={{0,2},{1,5},{2,0},{3,7},{4,6},{5,1},{6,4},{7,3},{8,10},{9,13},{10,... | collective-permute-start | bytes 4915208 | tf_op jit(solution)/shard_map/ppermute | solution.py:585
  98.7 36.9 %collective-permute-start.7 = (bf16[640,1280]{1,0:T(8,128)(2,1)}, bf16[640,1280]{1,0:T(8,128)(2,1)}, u32[]{:S(2)}, u32[]{:S(2)}) collective-permute-start(bf16[640,1280]{1,0:T(8,128)(2,1)} %collective-permute-done.3.refs_2_), channel_id=1, source_target_pairs={{0,1},{1,0},{2,3},{3,2},{4,5},{5,4},{6,7},{7,6},{8,9},{9,8},{10,11... | collective-permute-start | bytes 4915208 | tf_op jit(solution)/shard_map/ppermute | solution.py:585
  100.6 35.1 %collective-permute-start.9 = (bf16[640,1280]{1,0:T(8,128)(2,1)}, bf16[640,1280]{1,0:T(8,128)(2,1)}, u32[]{:S(2)}, u32[]{:S(2)}) collective-permute-start(bf16[640,1280]{1,0:T(8,128)(2,1)} %collective-permute-done.5.refs_6_), channel_id=1, source_target_pairs={{0,1},{1,0},{2,3},{3,2},{4,5},{5,4},{6,7},{7,6},{8,9},{9,8},{10,11... | collective-permute-start | bytes 4915208 | tf_op jit(solution)/shard_map/ppermute | solution.py:585
  134.4 37.6 %collective-permute-start.11 = (bf16[1280,640]{1,0:T(8,128)(2,1)}, bf16[1280,640]{1,0:T(8,128)(2,1)S(1)}, u32[]{:S(2)}, u32[]{:S(2)}) collective-permute-start(bf16[1280,640]{1,0:T(8,128)(2,1)} %collective-permute-done.10.refs_0_.refs_8_), channel_id=1, source_target_pairs={{0,1},{1,0},{2,3},{3,2},{4,5},{5,4},{6,7},{7,6},{8,9},{9,8},{10,11... | collective-permute-start | bytes 4915208 | tf_op jit(solution)/shard_map/ppermute | solution.py:585
  135.7 36.4 %collective-permute-start.13 = (bf16[640,1280]{1,0:T(8,128)(2,1)}, bf16[640,1280]{1,0:T(8,128)(2,1)}, u32[]{:S(2)}, u32[]{:S(2)}) collective-permute-start(bf16[640,1280]{1,0:T(8,128)(2,1)} %collective-permute-done.12.refs_2_.refs_10_), channel_id=1, source_target_pairs={{0,1},{1,0},{2,3},{3,2},{4,5},{5,4},{6,7},{7,6},{8,9},{9,8},{10,11... | collective-permute-start | bytes 4915208 | tf_op jit(solution)/shard_map/ppermute | solution.py:585
  204.0 66.1 %collective-permute-start.16 = (f32[1024,1280]{1,0:T(8,128)}, f32[1024,1280]{1,0:T(8,128)}, u32[]{:S(2)}, u32[]{:S(2)}) collective-permute-start(f32[1024,1280]{1,0:T(8,128)} %get-tuple-element.101.refs_12_.x2.refs_0_), channel_id=1, source_target_pairs={{0,1},{1,0},{2,3},{3,2},{4,5},{5,4},{6,7},{7,6},{8,9},{9,8},{10,11... | collective-permute-start | bytes 15728648 | tf_op jit(solution)/shard_map/ppermute | solution.py:585
  204.6 66.1 %collective-permute-start.17 = (f32[1024,1280]{1,0:T(8,128)}, f32[1024,1280]{1,0:T(8,128)}, u32[]{:S(2)}, u32[]{:S(2)}) collective-permute-start(f32[1024,1280]{1,0:T(8,128)} %get-tuple-element.105.d1), channel_id=1, source_target_pairs={{0,1},{1,0},{2,3},{3,2},{4,5},{5,4},{6,7},{7,6},{8,9},{9,8},{10,11... | collective-permute-start | bytes 15728648 | tf_op jit(solution)/shard_map/ppermute | solution.py:585
  204.7 149.4 %collective-permute-start.33 = (bf16[160,1280]{1,0:T(8,128)(2,1)}, bf16[160,1280]{1,0:T(8,128)(2,1)S(1)}, u32[]{:S(2)}, u32[]{:S(2)}) collective-permute-start(bf16[160,1280]{1,0:T(8,128)(2,1)} %bitcast.24.wo.refs_8_), channel_id=1, source_target_pairs={{0,4},{1,3},{2,6},{3,1},{4,0},{5,7},{6,2},{7,5},{8,12},{9,11},{10,... | collective-permute-start | bytes 1228808 | tf_op jit(solution)/shard_map/ppermute | solution.py:585
  206.7 193.0 %collective-permute-start.32 = (bf16[160,1280]{1,0:T(8,128)(2,1)}, bf16[160,1280]{1,0:T(8,128)(2,1)}, u32[]{:S(2)}, u32[]{:S(2)}) collective-permute-start(bf16[160,1280]{1,0:T(8,128)(2,1)} %bitcast.24.wo.refs_8_), channel_id=1, source_target_pairs={{0,2},{1,5},{2,0},{3,7},{4,6},{5,1},{6,4},{7,3},{8,10},{9,13},{10,... | collective-permute-start | bytes 1228808 | tf_op jit(solution)/shard_map/ppermute | solution.py:585
  270.1 107.2 %collective-permute-start.14 = (f32[1024,1280]{1,0:T(8,128)}, f32[1024,1280]{1,0:T(8,128)}, u32[]{:S(2)}, u32[]{:S(2)}) collective-permute-start(f32[1024,1280]{1,0:T(8,128)} %get-tuple-element.102.refs_0_.x2.refs_2_), channel_id=1, source_target_pairs={{0,1},{1,0},{2,3},{3,2},{4,5},{5,4},{6,7},{7,6},{8,9},{9,8},{10,11... | collective-permute-start | bytes 15728648 | tf_op jit(solution)/shard_map/ppermute | solution.py:585
  270.2 107.2 %collective-permute-start.15 = (f32[1024,1280]{1,0:T(8,128)}, f32[1024,1280]{1,0:T(8,128)}, u32[]{:S(2)}, u32[]{:S(2)}) collective-permute-start(f32[1024,1280]{1,0:T(8,128)} %get-tuple-element.103.d1), channel_id=1, source_target_pairs={{0,1},{1,0},{2,3},{3,2},{4,5},{5,4},{6,7},{7,6},{8,9},{9,8},{10,11... | collective-permute-start | bytes 15728648 | tf_op jit(solution)/shard_map/ppermute | solution.py:585
  291.9 62.7 %collective-permute-start.18 = (bf16[1024,1280]{1,0:T(8,128)(2,1)}, bf16[1024,1280]{1,0:T(8,128)(2,1)}, u32[]{:S(2)}, u32[]{:S(2)}) collective-permute-start(bf16[1024,1280]{1,0:T(8,128)(2,1)} %get-tuple-element.106.refs_12_), channel_id=1, source_target_pairs={{0,1},{1,0},{2,3},{3,2},{4,5},{5,4},{6,7},{7,6},{8,9},{9,8},{10,11... | collective-permute-start | bytes 7864328 | tf_op jit(solution)/shard_map/ppermute | solution.py:585
  354.1 45.7 %collective-permute-start.35 = (bf16[160,1280]{1,0:T(8,128)(2,1)}, bf16[160,1280]{1,0:T(8,128)(2,1)S(1)}, u32[]{:S(2)}, u32[]{:S(2)}) collective-permute-start(bf16[160,1280]{1,0:T(8,128)(2,1)} %bitcast.24.wo.refs_8_), channel_id=1, source_target_pairs={{0,1},{1,0},{2,3},{3,2},{4,5},{5,4},{6,7},{7,6},{8,9},{9,8},{10,11... | collective-permute-start | bytes 1228808 | tf_op jit(solution)/shard_map/ppermute | solution.py:585
  354.6 45.6 %collective-permute-start.34 = (bf16[160,1280]{1,0:T(8,128)(2,1)S(1)}, bf16[160,1280]{1,0:T(8,128)(2,1)S(1)}, u32[]{:S(2)}, u32[]{:S(2)}) collective-permute-start(bf16[160,1280]{1,0:T(8,128)(2,1)S(1)} %collective-permute-done.33.refs_10_), channel_id=1, source_target_pairs={{0,2},{1,5},{2,0},{3,7},{4,6},{5,1},{6,4},{7,3},{8,10},{9,13},{10,... | collective-permute-start | bytes 1228808 | tf_op jit(solution)/shard_map/ppermute | solution.py:585
  377.3 111.3 %collective-permute-start.21 = (f32[1024,1280]{1,0:T(8,128)}, f32[1024,1280]{1,0:T(8,128)}, u32[]{:S(2)}, u32[]{:S(2)}) collective-permute-start(f32[1024,1280]{1,0:T(8,128)} %get-tuple-element.112.refs_6_.x2.refs_0_), channel_id=1, source_target_pairs={{0,1},{1,0},{2,3},{3,2},{4,5},{5,4},{6,7},{7,6},{8,9},{9,8},{10,11... | collective-permute-start | bytes 15728648 | tf_op jit(solution)/shard_map/ppermute | solution.py:585
  377.4 111.3 %collective-permute-start.22 = (f32[1024,1280]{1,0:T(8,128)}, f32[1024,1280]{1,0:T(8,128)}, u32[]{:S(2)}, u32[]{:S(2)}) collective-permute-start(f32[1024,1280]{1,0:T(8,128)} %get-tuple-element.121.d1), channel_id=1, source_target_pairs={{0,1},{1,0},{2,3},{3,2},{4,5},{5,4},{6,7},{7,6},{8,9},{9,8},{10,11... | collective-permute-start | bytes 15728648 | tf_op jit(solution)/shard_map/ppermute | solution.py:585
  399.7 63.1 %collective-permute-start.37 = (bf16[160,1280]{1,0:T(8,128)(2,1)S(1)}, bf16[160,1280]{1,0:T(8,128)(2,1)S(1)}, u32[]{:S(2)}, u32[]{:S(2)}) collective-permute-start(bf16[160,1280]{1,0:T(8,128)(2,1)S(1)} %collective-permute-done.33.refs_10_), channel_id=1, source_target_pairs={{0,1},{1,0},{2,3},{3,2},{4,5},{5,4},{6,7},{7,6},{8,9},{9,8},{10,11... | collective-permute-start | bytes 1228808 | tf_op jit(solution)/shard_map/ppermute | solution.py:585
  399.8 62.5 %collective-permute-start.36 = (bf16[160,1280]{1,0:T(8,128)(2,1)}, bf16[160,1280]{1,0:T(8,128)(2,1)}, u32[]{:S(2)}, u32[]{:S(2)}) collective-permute-start(bf16[160,1280]{1,0:T(8,128)(2,1)} %collective-permute-done.32.refs_9_), channel_id=1, source_target_pairs={{0,1},{1,0},{2,3},{3,2},{4,5},{5,4},{6,7},{7,6},{8,9},{9,8},{10,11... | collective-permute-start | bytes 1228808 | tf_op jit(solution)/shard_map/ppermute | solution.py:585
  400.2 63.4 %collective-permute-start.23 = (bf16[1024,1280]{1,0:T(8,128)(2,1)}, bf16[1024,1280]{1,0:T(8,128)(2,1)}, u32[]{:S(2)}, u32[]{:S(2)}) collective-permute-start(bf16[1024,1280]{1,0:T(8,128)(2,1)} %get-tuple-element.118.refs_12_), channel_id=1, source_target_pairs={{0,1},{1,0},{2,3},{3,2},{4,5},{5,4},{6,7},{7,6},{8,9},{9,8},{10,11... | collective-permute-start | bytes 7864328 | tf_op jit(solution)/shard_map/ppermute | solution.py:585
  487.7 85.1 %collective-permute-start.19 = (f32[1024,1280]{1,0:T(8,128)}, f32[1024,1280]{1,0:T(8,128)}, u32[]{:S(2)}, u32[]{:S(2)}) collective-permute-start(f32[1024,1280]{1,0:T(8,128)} %get-tuple-element.119.refs_6_.x2.refs_0_), channel_id=1, source_target_pairs={{0,1},{1,0},{2,3},{3,2},{4,5},{5,4},{6,7},{7,6},{8,9},{9,8},{10,11... | collective-permute-start | bytes 15728648 | tf_op jit(solution)/shard_map/ppermute | solution.py:585
  488.6 85.8 %collective-permute-start.20 = (f32[1024,1280]{1,0:T(8,128)}, f32[1024,1280]{1,0:T(8,128)}, u32[]{:S(2)}, u32[]{:S(2)}) collective-permute-start(f32[1024,1280]{1,0:T(8,128)} %get-tuple-element.120.d1), channel_id=1, source_target_pairs={{0,1},{1,0},{2,3},{3,2},{4,5},{5,4},{6,7},{7,6},{8,9},{9,8},{10,11... | collective-permute-start | bytes 15728648 | tf_op jit(solution)/shard_map/ppermute | solution.py:585
  511.7 36.8 %collective-permute-start.24 = (bf16[1024,1280]{1,0:T(8,128)(2,1)}, bf16[1024,1280]{1,0:T(8,128)(2,1)}, u32[]{:S(2)}, u32[]{:S(2)}) collective-permute-start(bf16[1024,1280]{1,0:T(8,128)(2,1)} %get-tuple-element.132.refs_16_), channel_id=1, source_target_pairs={{0,1},{1,0},{2,3},{3,2},{4,5},{5,4},{6,7},{7,6},{8,9},{9,8},{10,11... | collective-permute-start | bytes 7864328 | tf_op jit(solution)/shard_map/ppermute | solution.py:585
  519.3 53.0 %collective-permute-start.98 = (f32[640,1280]{1,0:T(8,128)}, f32[640,1280]{1,0:T(8,128)}, u32[]{:S(2)}, u32[]{:S(2)}) collective-permute-start(f32[640,1280]{1,0:T(8,128)} %get-tuple-element.163), channel_id=1, source_target_pairs={{0,1},{1,0},{2,3},{3,2},{4,5},{5,4},{6,7},{7,6},{8,9},{9,8},{10,11... | collective-permute-start | bytes 9830408 | tf_op jit(solution)/shard_map/ppermute | solution.py:585
  531.5 65.4 %collective-permute-start.97 = (f32[1280,640]{1,0:T(8,128)}, f32[1280,640]{1,0:T(8,128)}, u32[]{:S(2)}, u32[]{:S(2)}) collective-permute-start(f32[1280,640]{1,0:T(8,128)} %get-tuple-element.162), channel_id=1, source_target_pairs={{0,1},{1,0},{2,3},{3,2},{4,5},{5,4},{6,7},{7,6},{8,9},{9,8},{10,11... | collective-permute-start | bytes 9830408 | tf_op jit(solution)/shard_map/ppermute | solution.py:585
  548.5 48.5 %collective-permute-start.64 = (bf16[256,1280]{1,0:T(8,128)(2,1)S(1)}, bf16[256,1280]{1,0:T(8,128)(2,1)}, u32[]{:S(2)}, u32[]{:S(2)}) collective-permute-start(bf16[256,1280]{1,0:T(8,128)(2,1)S(1)} %fusion.3.refs_4_), channel_id=1, source_target_pairs={{0,4},{1,3},{2,6},{3,1},{4,0},{5,7},{6,2},{7,5},{8,12},{9,11},{10,... | collective-permute-start | bytes 1966088 | tf_op jit(solution)/shard_map/ppermute | solution.py:585
  596.9 57.6 %collective-permute-start.39 = (bf16[1024,1280]{1,0:T(8,128)(2,1)}, bf16[1024,1280]{1,0:T(8,128)(2,1)}, u32[]{:S(2)}, u32[]{:S(2)}) collective-permute-start(bf16[1024,1280]{1,0:T(8,128)(2,1)} %get-tuple-element.144.refs_16_), channel_id=1, source_target_pairs={{0,1},{1,0},{2,3},{3,2},{4,5},{5,4},{6,7},{7,6},{8,9},{9,8},{10,11... | collective-permute-start | bytes 7864328 | tf_op jit(solution)/shard_map/ppermute | solution.py:585
  653.4 39.1 %collective-permute-start.75 = (bf16[256,1280]{1,0:T(8,128)(2,1)S(1)}, bf16[256,1280]{1,0:T(8,128)(2,1)}, u32[]{:S(2)}, u32[]{:S(2)}) collective-permute-start(bf16[256,1280]{1,0:T(8,128)(2,1)S(1)} %fusion.2.refs_12_), channel_id=1, source_target_pairs={{0,1},{1,0},{2,3},{3,2},{4,5},{5,4},{6,7},{7,6},{8,9},{9,8},{10,11... | collective-permute-start | bytes 1966088 | tf_op jit(solution)/shard_map/ppermute | solution.py:585
  653.4 36.9 %collective-permute-start.88 = (bf16[512,1280]{1,0:T(8,128)(2,1)}, bf16[512,1280]{1,0:T(8,128)(2,1)}, u32[]{:S(2)}, u32[]{:S(2)}) collective-permute-start(bf16[512,1280]{1,0:T(8,128)(2,1)} %get-tuple-element.143.refs_4_), channel_id=1, source_target_pairs={{0,2},{1,5},{2,0},{3,7},{4,6},{5,1},{6,4},{7,3},{8,10},{9,13},{10,... | collective-permute-start | bytes 3932168 | tf_op jit(solution)/shard_map/ppermute | solution.py:585
  654.5 39.6 %collective-permute-start.55 = (bf16[160,2048]{1,0:T(8,128)(2,1)S(1)}, bf16[160,2048]{1,0:T(8,128)(2,1)}, u32[]{:S(2)}, u32[]{:S(2)}) collective-permute-start(bf16[160,2048]{1,0:T(8,128)(2,1)S(1)} %copy-done.18), channel_id=1, source_target_pairs={{0,4},{1,3},{2,6},{3,1},{4,0},{5,7},{6,2},{7,5},{8,12},{9,11},{10,... | collective-permute-start | bytes 1966088 | tf_op jit(solution)/shard_map/ppermute | solution.py:585
  690.3 42.1 %collective-permute-start.79 = (bf16[512,1280]{1,0:T(8,128)(2,1)}, bf16[512,1280]{1,0:T(8,128)(2,1)S(1)}, u32[]{:S(2)}, u32[]{:S(2)}) collective-permute-start(bf16[512,1280]{1,0:T(8,128)(2,1)} %get-tuple-element.155.refs_21_), channel_id=1, source_target_pairs={{0,2},{1,5},{2,0},{3,7},{4,6},{5,1},{6,4},{7,3},{8,10},{9,13},{10,... | collective-permute-start | bytes 3932168 | tf_op jit(solution)/shard_map/ppermute | solution.py:585
  698.2 34.2 %collective-permute-start.56 = (bf16[160,2048]{1,0:T(8,128)(2,1)}, bf16[160,2048]{1,0:T(8,128)(2,1)S(1)}, u32[]{:S(2)}, u32[]{:S(2)}) collective-permute-start(bf16[160,2048]{1,0:T(8,128)(2,1)} %collective-permute-done.55.refs_2_), channel_id=1, source_target_pairs={{0,2},{1,5},{2,0},{3,7},{4,6},{5,1},{6,4},{7,3},{8,10},{9,13},{10,... | collective-permute-start | bytes 1966088 | tf_op jit(solution)/shard_map/ppermute | solution.py:585
  735.5 36.5 %collective-permute-start.48 = (bf16[160,2048]{1,0:T(8,128)(2,1)}, bf16[160,2048]{1,0:T(8,128)(2,1)}, u32[]{:S(2)}, u32[]{:S(2)}) collective-permute-start(bf16[160,2048]{1,0:T(8,128)(2,1)} %get-tuple-element.151.refs_0_), channel_id=1, source_target_pairs={{0,4},{1,3},{2,6},{3,1},{4,0},{5,7},{6,2},{7,5},{8,12},{9,11},{10,... | collective-permute-start | bytes 1966088 | tf_op jit(solution)/shard_map/ppermute | solution.py:585
  783.0 61.2 %collective-permute-start.52 = (bf16[160,2048]{1,0:T(8,128)(2,1)}, bf16[160,2048]{1,0:T(8,128)(2,1)}, u32[]{:S(2)}, u32[]{:S(2)}) collective-permute-start(bf16[160,2048]{1,0:T(8,128)(2,1)} %collective-permute-done.48.refs_2_), channel_id=1, source_target_pairs={{0,1},{1,0},{2,3},{3,2},{4,5},{5,4},{6,7},{7,6},{8,9},{9,8},{10,11... | collective-permute-start | bytes 1966088 | tf_op jit(solution)/shard_map/ppermute | solution.py:585
  783.1 44.7 %collective-permute-start.51 = (bf16[160,2048]{1,0:T(8,128)(2,1)}, bf16[160,2048]{1,0:T(8,128)(2,1)}, u32[]{:S(2)}, u32[]{:S(2)}) collective-permute-start(bf16[160,2048]{1,0:T(8,128)(2,1)} %collective-permute-done.47.refs_1_), channel_id=1, source_target_pairs={{0,1},{1,0},{2,3},{3,2},{4,5},{5,4},{6,7},{7,6},{8,9},{9,8},{10,11... | collective-permute-start | bytes 1966088 | tf_op jit(solution)/shard_map/ppermute | solution.py:585
  793.3 51.6 %collective-permute-start.53 = (bf16[160,2048]{1,0:T(8,128)(2,1)}, bf16[160,2048]{1,0:T(8,128)(2,1)}, u32[]{:S(2)}, u32[]{:S(2)}) collective-permute-start(bf16[160,2048]{1,0:T(8,128)(2,1)} %collective-permute-done.49.refs_3_), channel_id=1, source_target_pairs={{0,1},{1,0},{2,3},{3,2},{4,5},{5,4},{6,7},{7,6},{8,9},{9,8},{10,11... | collective-permute-start | bytes 1966088 | tf_op jit(solution)/shard_map/ppermute | solution.py:585
  793.3 51.6 %collective-permute-start.81 = (bf16[256,1280]{1,0:T(8,128)(2,1)S(1)}, bf16[256,1280]{1,0:T(8,128)(2,1)}, u32[]{:S(2)}, u32[]{:S(2)}) collective-permute-start(bf16[256,1280]{1,0:T(8,128)(2,1)S(1)} %fusion.1.refs_2_), channel_id=1, source_target_pairs={{0,2},{1,5},{2,0},{3,7},{4,6},{5,1},{6,4},{7,3},{8,10},{9,13},{10,... | collective-permute-start | bytes 1966088 | tf_op jit(solution)/shard_map/ppermute | solution.py:585
  793.4 51.9 %collective-permute-start.83 = (bf16[256,1280]{1,0:T(8,128)(2,1)}, bf16[256,1280]{1,0:T(8,128)(2,1)}, u32[]{:S(2)}, u32[]{:S(2)}) collective-permute-start(bf16[256,1280]{1,0:T(8,128)(2,1)} %collective-permute-done.82.refs_4_), channel_id=1, source_target_pairs={{0,2},{1,5},{2,0},{3,7},{4,6},{5,1},{6,4},{7,3},{8,10},{9,13},{10,... | collective-permute-start | bytes 1966088 | tf_op jit(solution)/shard_map/ppermute | solution.py:585
  827.8 34.0 %collective-permute-start.96 = (bf16[256,1280]{1,0:T(8,128)(2,1)S(1)}, bf16[256,1280]{1,0:T(8,128)(2,1)}, u32[]{:S(2)}, u32[]{:S(2)}) collective-permute-start(bf16[256,1280]{1,0:T(8,128)(2,1)S(1)} %collective-permute-done.92.refs_5_), channel_id=1, source_target_pairs={{0,1},{1,0},{2,3},{3,2},{4,5},{5,4},{6,7},{7,6},{8,9},{9,8},{10,11... | collective-permute-start | bytes 1966088 | tf_op jit(solution)/shard_map/ppermute | solution.py:585
  844.3 35.6 %collective-permute-start.84 = (bf16[256,1280]{1,0:T(8,128)(2,1)S(1)}, bf16[256,1280]{1,0:T(8,128)(2,1)S(1)}, u32[]{:S(2)}, u32[]{:S(2)}) collective-permute-start(bf16[256,1280]{1,0:T(8,128)(2,1)S(1)} %fusion.1.refs_2_), channel_id=1, source_target_pairs={{0,1},{1,0},{2,3},{3,2},{4,5},{5,4},{6,7},{7,6},{8,9},{9,8},{10,11... | collective-permute-start | bytes 1966088 | tf_op jit(solution)/shard_map/ppermute | solution.py:585
  844.8 35.2 %collective-permute-start.86 = (bf16[256,1280]{1,0:T(8,128)(2,1)}, bf16[256,1280]{1,0:T(8,128)(2,1)}, u32[]{:S(2)}, u32[]{:S(2)}) collective-permute-start(bf16[256,1280]{1,0:T(8,128)(2,1)} %collective-permute-done.82.refs_4_), channel_id=1, source_target_pairs={{0,1},{1,0},{2,3},{3,2},{4,5},{5,4},{6,7},{7,6},{8,9},{9,8},{10,11... | collective-permute-start | bytes 1966088 | tf_op jit(solution)/shard_map/ppermute | solution.py:585
  844.9 35.1 %collective-permute-start.85 = (bf16[256,1280]{1,0:T(8,128)(2,1)}, bf16[256,1280]{1,0:T(8,128)(2,1)}, u32[]{:S(2)}, u32[]{:S(2)}) collective-permute-start(bf16[256,1280]{1,0:T(8,128)(2,1)} %collective-permute-done.81.refs_3_), channel_id=1, source_target_pairs={{0,1},{1,0},{2,3},{3,2},{4,5},{5,4},{6,7},{7,6},{8,9},{9,8},{10,11... | collective-permute-start | bytes 1966088 | tf_op jit(solution)/shard_map/ppermute | solution.py:585
  845.3 34.6 %collective-permute-start.87 = (bf16[256,1280]{1,0:T(8,128)(2,1)}, bf16[256,1280]{1,0:T(8,128)(2,1)}, u32[]{:S(2)}, u32[]{:S(2)}) collective-permute-start(bf16[256,1280]{1,0:T(8,128)(2,1)} %collective-permute-done.83.refs_5_), channel_id=1, source_target_pairs={{0,1},{1,0},{2,3},{3,2},{4,5},{5,4},{6,7},{7,6},{8,9},{9,8},{10,11... | collective-permute-start | bytes 1966088 | tf_op jit(solution)/shard_map/ppermute | solution.py:585
  (100 other events, 2258.9 us)
